TPU v7x, 32 devices: a whole 2x2x4 slice. The times are simulated.
32 devices in a mesh: rows: 8 (over z, x), grp: 4 (over y, core).
Axes of the slice: x: 2, y: 2, z: 4, core: 2. Of those that a mesh axis runs over, the one named last changes fastest.
Arguments:
- matrix: float32 [65536, 1024], P(('rows', 'grp'))
- row_signs: int32 [65536], P(('rows', 'grp')), may hold values from -1 to 1, as said below
- samples: int32 [8192], P(('rows', 'grp')), may hold values from 0 to 65535, as said below
Outputs:
- factor: float32 [1024, 1024], P('rows')
Inputs may be any that keep to these rules, and one draw needn't show every extreme that they name: `row_signs`: every entry is 1 or -1. `samples`: entries are distinct and increasing; entries k * 256 to (k + 1) * 256 - 1 lie in rows k * 2048 to (k + 1) * 2048 - 1.
All inputs are finite; a program needn't handle non-finite values.
Results may differ from a plain program's by a relative error of at most 0.00011.
Values sent between devices are 32-bit elements; how exact they have to be, the bound alone decides.
A program may use at most 128 MiB of HBM per device.

v0:
```python
import functools

import jax
import jax.numpy as jnp
from jax import lax
from jax.experimental import pallas as pl
from jax.experimental.pallas import tpu as pltpu
from jax.sharding import PartitionSpec as P

exact_mode = lax.Precision.HIGHEST
VMEM_LIMIT = 60 * 1024 * 1024
TILE = 128


def sylvester(length):
    matrix = jnp.ones((1, 1), jnp.float32)
    while matrix.shape[0] < length:
        matrix = jnp.block([[matrix, matrix], [matrix, -matrix]])
    return matrix


def butterfly(parts):
    span = 1
    while span < len(parts):
        parts = list(parts)
        for start in range(0, len(parts), 2 * span):
            for i in range(start, start + span):
                low, high = parts[i], parts[i + span]
                parts[i], parts[i + span] = low + high, low - high
        span *= 2
    return parts


def split(x):
    high = x.astype(jnp.bfloat16)
    return high, (x - high.astype(jnp.float32)).astype(jnp.bfloat16)


def local_kernel(base, x_ref, s_ref, h_ref, o_ref):
    parts = []
    for i in range(x_ref.shape[0] // base):
        rows = slice(i * base, (i + 1) * base)
        high, low = split(x_ref[rows, :] * s_ref[rows, :])
        both = jnp.dot(h_ref[...], high, preferred_element_type=jnp.float32)
        both += jnp.dot(h_ref[...], low, preferred_element_type=jnp.float32)
        parts.append(both)
    for i, part in enumerate(butterfly(parts)):
        o_ref[i * base : (i + 1) * base, :] = part


def local_transform(matrix, signs, base):
    rows, cols = matrix.shape
    return pl.pallas_call(
        functools.partial(local_kernel, base),
        grid=(cols // TILE,),
        out_shape=jax.ShapeDtypeStruct((rows, cols), jnp.float32),
        in_specs=[
            pl.BlockSpec((rows, TILE), lambda c: (0, c)),
            pl.BlockSpec((rows, TILE), lambda c: (0, 0)),
            pl.BlockSpec((base, base), lambda c: (0, 0)),
        ],
        out_specs=pl.BlockSpec((rows, TILE), lambda c: (0, c)),
        compiler_params=pltpu.CompilerParams(vmem_limit_bytes=VMEM_LIMIT),
    )(matrix, signs, sylvester(base).astype(jnp.bfloat16))


def gram_kernel(scale, x_ref, w_ref, o_ref, left, right):
    blocks, step, cols = x_ref.shape
    rows = blocks * step

    @pl.when(pl.program_id(0) == 0)
    def _():
        o_ref[...] = jnp.zeros_like(o_ref)

    def mix(c, carry):
        at = pl.ds(pl.multiple_of(c * TILE, TILE), TILE)
        parts = butterfly([x_ref[b, :, at] for b in range(blocks)])
        for b in range(0, blocks, 2):
            x = jnp.concatenate(parts[b : b + 2], axis=0) * scale
            w = jnp.concatenate([w_ref[b], w_ref[b + 1]], axis=0)
            high, low = split(x)
            here = slice(b * step, (b + 2) * step)
            there = slice(rows + b * step, rows + (b + 2) * step)
            masked = (high.astype(jnp.float32) * w).astype(jnp.bfloat16)
            left[here, at] = masked
            right[here, at] = high
            left[there, at] = masked
            right[there, at] = (2.0 * low.astype(jnp.float32)).astype(jnp.bfloat16)
        return carry

    lax.fori_loop(0, cols // TILE, mix, 0)
    wide = 2 * TILE

    def add(n, carry):
        at = pl.ds(pl.multiple_of(n * wide, wide), wide)
        o_ref[:, at] += lax.dot_general(
            left[...], right[:, at], (((0,), (0,)), ((), ())), preferred_element_type=jnp.float32
        )
        return carry

    lax.fori_loop(0, cols // wide, add, 0)


def gram_share(arrived, weights, scale):
    blocks, piece, cols = arrived.shape
    step = 8
    return pl.pallas_call(
        functools.partial(gram_kernel, scale),
        grid=(piece // step,),
        out_shape=jax.ShapeDtypeStruct((cols, cols), jnp.float32),
        in_specs=[
            pl.BlockSpec((blocks, step, cols), lambda t: (0, t, 0)),
            pl.BlockSpec((blocks, step, TILE), lambda t: (0, t, 0)),
        ],
        out_specs=pl.BlockSpec((cols, cols), lambda t: (0, 0)),
        scratch_shapes=[pltpu.VMEM((2 * blocks * step, cols), jnp.bfloat16)] * 2,
        compiler_params=pltpu.CompilerParams(vmem_limit_bytes=VMEM_LIMIT),
    )(arrived, weights)


def upper_tiles(cols):
    return [(i, j) for i in range(0, cols, TILE) for j in range(i, cols, TILE)]


def factor_kernel(g_ref, u_ref, work):
    cols = u_ref.shape[0]
    work[...] = jnp.zeros_like(work)
    for p, (i, j) in enumerate(upper_tiles(cols)):
        work[i : i + TILE, j : j + TILE] = g_ref[p * TILE : (p + 1) * TILE, :]
    row_id = lax.broadcasted_iota(jnp.int32, (TILE, TILE), 0)
    lane_id = lax.broadcasted_iota(jnp.int32, (TILE, TILE), 1)

    def panel(k, carry):
        base = pl.multiple_of(k * TILE, TILE)
        here = pl.ds(base, TILE)
        block = work[here, here]
        strips = [block[i : i + 8, :] for i in range(0, TILE, 8)]
        unit = (row_id == lane_id).astype(jnp.float32)
        inverse = [unit[i : i + 8, :] for i in range(0, TILE, 8)]
        sub_id = lax.broadcasted_iota(jnp.int32, (8, TILE), 0)
        for j in range(TILE):
            s, r = divmod(j, 8)
            row = strips[s][r : r + 1, :]
            inv_row = inverse[s][r : r + 1, :]
            root = lax.rsqrt(jnp.broadcast_to(row[:, j : j + 1], (1, TILE)))
            row = row * root
            inv_row = inv_row * root
            for i in range(s, TILE // 8):
                column = jnp.broadcast_to(strips[i][:, j : j + 1], (8, TILE)) * root
                if i == s:
                    column = jnp.where(sub_id > r, column, 0.0)
                strips[i] = strips[i] - column * row
                inverse[i] = inverse[i] - column * inv_row
                if i == s:
                    inverse[i] = jnp.where(sub_id == r, inv_row, inverse[i])
        lower_inverse = jnp.concatenate(inverse, axis=0)
        lower_inverse = jnp.where(lane_id <= row_id, lower_inverse, 0.0)
        wide_row = lax.broadcasted_iota(jnp.int32, (TILE, cols), 0) + base
        wide_lane = lax.broadcasted_iota(jnp.int32, (TILE, cols), 1)
        upper = jnp.dot(
            lower_inverse, work[here, :], precision=exact_mode, preferred_element_type=jnp.float32
        )
        u_ref[here, :] = jnp.where(wide_lane >= wide_row, upper, 0.0)

        def trail(i, inner):
            there = pl.ds(pl.multiple_of(i * TILE, TILE), TILE)
            work[there, :] -= lax.dot_general(
                u_ref[here, there],
                u_ref[here, :],
                (((0,), (0,)), ((), ())),
                precision=exact_mode,
                preferred_element_type=jnp.float32,
            )
            return inner

        lax.fori_loop(k + 1, cols // TILE, trail, 0)
        return carry

    lax.fori_loop(0, cols // TILE, panel, 0)


def factorize(packed, cols):
    return pl.pallas_call(
        factor_kernel,
        out_shape=jax.ShapeDtypeStruct((cols, cols), jnp.float32),
        in_specs=[pl.BlockSpec(memory_space=pltpu.VMEM)],
        out_specs=pl.BlockSpec(memory_space=pltpu.VMEM),
        scratch_shapes=[pltpu.VMEM((cols, cols), jnp.float32)],
        compiler_params=pltpu.CompilerParams(vmem_limit_bytes=VMEM_LIMIT),
    )(packed)


def shards(matrix, row_signs, samples):
    count_rows = lax.axis_size("rows")
    blocks = count_rows * lax.axis_size("grp")
    row_dev, col_count = matrix.shape
    piece_rows = row_dev // blocks
    sample_dev = samples.shape[0]
    position = lax.axis_index(("rows", "grp"))
    all_indices = lax.all_gather(samples, ("rows", "grp"), axis=0)
    signs = jnp.broadcast_to(row_signs.astype(jnp.float32)[:, None], (row_dev, TILE))
    before = local_transform(matrix, signs, min(256, row_dev))
    arrived = lax.all_to_all(
        before.reshape(blocks, piece_rows, col_count),
        ("rows", "grp"),
        split_axis=0,
        concat_axis=0,
        tiled=True,
    )
    first = jnp.arange(blocks, dtype=jnp.int32)[:, None] * row_dev + position * piece_rows
    within = all_indices - first
    hits = within[:, None, :] == jnp.arange(piece_rows, dtype=jnp.int32)[None, :, None]
    weights = jnp.max(hits.astype(jnp.float32), axis=2)
    weights = jnp.broadcast_to(weights[:, :, None], (blocks, piece_rows, TILE))
    scale = (sample_dev * blocks) ** -0.5
    half = gram_share(arrived, weights, scale)
    whole = (half + half.T) * 0.5
    packed = jnp.concatenate(
        [whole[i : i + TILE, j : j + TILE] for i, j in upper_tiles(col_count)], axis=0
    )
    summed = lax.psum(packed, ("rows", "grp"))
    upper_factor = factorize(summed, col_count)
    share_rows = col_count // count_rows
    return lax.dynamic_slice_in_dim(
        upper_factor, lax.axis_index("rows") * share_rows, share_rows, 0
    )


def solution(mesh):
    return jax.shard_map(
        shards,
        mesh=mesh,
        in_specs=(P(("rows", "grp"), None), P(("rows", "grp")), P(("rows", "grp"))),
        out_specs=P("rows", None),
        check_vma=False,
    )
```

profile of v0, /device:TPU:0, one launch (start us, length us, event | category | flops | bytes accessed | tf_op | source)
XLA Modules:
  0.0 536.0 jit_solution(18233841418340778915)
XLA Ops:
  6.5 0.7 convert_element_type.7
  7.2 1.3 broadcast_in_dim.4.s_ref
  8.5 11.3 %shard_map.37 = f32[2048,1024]{1,0:T(8,128)} custom-call(f32[2048,1024]{1,0:T(8,128)} %x_ref.1, f32[2048,128]{1,0:T(8,128)} %broadcast_in_dim.4.s_ref, bf16[256,256]{1,0:T(8,128)(2,1)} %constant.48.clone.1.h_ref), custom_call_target="tpu_custom_call" | custom-call | tf_op jit(solution)/shard_map/pallas_call | solution.py:53
  19.9 0.0 copy-start.1
  19.9 7.4 %all-to-all-start = ((f32[32,64,1024]{2,1,0:T(8,128)}), f32[32,64,1024]{2,1,0:T(8,128)}, u32[]{:S(2)}, u32[]{:S(2)}) async-start(f32[32,64,1024]{2,1,0:T(8,128)} %bitcast.8), calls=%async_computation | async-start | bytes 16777216 | tf_op jit(solution)/shard_map/all_to_all | solution.py:203
  27.3 0.0 all-reduce.2.cloned.1.call-start
  27.4 0.0 copy-done.1
  27.4 177.0 %all-gather.1 = s32[32,1,256]{2,1,0:T(1,128)S(1)} all-gather(s32[1,1,256]{2,1,0:T(1,128)S(1)} %bitcast.9), channel_id=2, replica_groups=mesh['rows'=8,'grp'=4] {'rows','grp'}, dimensions={0}, use_global_device_ids=true | all-gather | bytes 33792 | tf_op jit(solution)/shard_map/all_gather | solution.py:200
  204.4 0.1 bitcast_subtract_fusion
  204.4 0.3 convert_reduce_fusion
  204.8 7.7 %all-to-all-done.x_ref = f32[32,64,1024]{2,1,0:T(8,128)} async-done(((f32[32,64,1024]{2,1,0:T(8,128)}), f32[32,64,1024]{2,1,0:T(8,128)}, u32[]{:S(2)}, u32[]{:S(2)}) %all-to-all-start) | async-done | bytes 8388640 | tf_op jit(solution)/shard_map/all_to_all | solution.py:203
  212.5 1.4 broadcast_in_dim.5.w_ref
  213.9 27.5 %shard_map.38 = f32[1024,1024]{1,0:T(8,128)} custom-call(f32[32,64,1024]{2,1,0:T(8,128)} %all-to-all-done.x_ref, f32[32,64,128]{2,1,0:T(8,128)} %broadcast_in_dim.5.w_ref), custom_call_target="tpu_custom_call" | custom-call | tf_op jit(solution)/shard_map/pallas_call | solution.py:107
  241.4 5.3 copy.6
  246.8 4.4 fusion
  251.9 0.0 copy-start
  251.9 1.4 copy-done
  253.3 0.0 all-reduce.2.cloned.1.call-update
  253.3 162.7 %all-reduce.2.cloned.1.call-done.g_ref = f32[4608,128]{1,0:T(8,128)} async-done(((f32[4608,128]{1,0:T(8,128)}), f32[4608,128]{1,0:T(8,128)}) %all-reduce.2.cloned.1.call-update) | async-done | bytes 2359312 | tf_op jit(solution)/shard_map/psum | solution.py:221
  416.0 111.3 %shard_map.39 = f32[1024,1024]{1,0:T(8,128)} custom-call(f32[4608,128]{1,0:T(8,128)} %all-reduce.2.cloned.1.call-done.g_ref), custom_call_target="tpu_custom_call" | custom-call | tf_op jit(solution)/shard_map/pallas_call | solution.py:183
  527.3 1.9 constant_dynamic-slice_fusion
  (36 shorter events, 0.4 us)
Async XLA Ops:
  19.9 7.5 %copy-start.1 = (s32[256]{0:T(256)S(1)}, s32[256]{0:T(256)}, u32[]{:S(2)}) copy-start(s32[256]{0:T(256)} %param.5) | copy-start | bytes 3076
  19.9 192.6 %all-to-all-start = ((f32[32,64,1024]{2,1,0:T(8,128)}), f32[32,64,1024]{2,1,0:T(8,128)}, u32[]{:S(2)}, u32[]{:S(2)}) async-start(f32[32,64,1024]{2,1,0:T(8,128)} %bitcast.8), calls=%async_computation | async-start | bytes 16777216 | tf_op jit(solution)/shard_map/all_to_all | solution.py:203
  27.3 388.7 %all-reduce.2.cloned.1.call-start = ((), (), s32[]{:S(2)}) async-start(), calls=%async_computation.1 | async-start | bytes 4718592 | tf_op jit(solution)/shard_map/psum | solution.py:221
  251.9 1.4 copy-start
Sparse Core Ops, SparseCore 0:
  253.4 162.5 all-reduce.1
where the time goes:
time: 537 us; the launch traced here: 536 us
  blocking collectives  177 us (33%)
  waiting for transfers between devices  170 us (32%)
  Pallas kernels  150 us (28%)
  between operations  13.7 us (3%)
  local copies, waits for them, and re-layouts  11.7 us (2%)
  starting transfers between devices  7.49 us (1%)
  other arithmetic  5.56 us (1%)
    all_gather x1, blocking collectives, shards(): all_indices = lax.all_gather(samples, ('rows', 'grp'), axis=0)  177 us
    psum x1, waiting for transfers between devices, shards(): summed = lax.psum(packed, ('rows', 'grp'))  163 us
    pallas_call x1, Pallas kernels, factorize(): pl.pallas_call(factor_kernel, out_shape=jax.ShapeDtypeStruct((cols, cols)...  111 us
    pallas_call x1, Pallas kernels, gram_share(): pl.pallas_call(functools.partial(gram_kernel, scale), grid=(piece // step...  27.5 us
    pallas_call x1, Pallas kernels, local_transform(): pl.pallas_call(functools.partial(local_kernel, base), grid=(cols // TILE,...  11.3 us
  transfers between devices with their start and end apart: 2, of which 2 were waited for; matrix products, arithmetic and copies ran while one was open for 0% of the time, Pallas kernels for 0%

commit v1 on v0

--- a/solution.py
+++ b/solution.py
@@ -7,7 +7,7 @@
 from jax.experimental.pallas import tpu as pltpu
 from jax.sharding import PartitionSpec as P
 
-exact_mode = lax.Precision.HIGHEST
+MESH = pl.DeviceIdType.MESH
 VMEM_LIMIT = 60 * 1024 * 1024
 TILE = 128
 
@@ -118,75 +118,277 @@
     )(arrived, weights)
 
 
-def upper_tiles(cols):
-    return [(i, j) for i in range(0, cols, TILE) for j in range(i, cols, TILE)]
-
-
-def factor_kernel(g_ref, u_ref, work):
+def panel_tiles(panels):
+    sizes = [panels - i + (panels - i) % 2 for i in range(panels)]
+    return sizes, [sum(sizes[:i]) for i in range(panels)]
+
+
+def segments(panels):
+    sizes, starts = panel_tiles(panels)
+    runs = [(0, 1), (1, 2), (2, 4), (4, panels)]
+    return [(starts[i], sum(sizes[i:j])) for i, j in runs]
+
+
+def dot3(a, b, dims):
+    (ah, al), (bh, bl) = a, b
+    go = functools.partial(lax.dot_general, dimension_numbers=(dims, ((), ())), preferred_element_type=jnp.float32)
+    return go(ah, bh) + (go(ah, bl) + go(al, bh))
+
+def spread(row):
+    return jnp.broadcast_to(row, (8, TILE))
+
+def factor_block(block, lines):
+    count, group = TILE // 8, 4
+    sub_id = lax.broadcasted_iota(jnp.int32, (8, TILE), 0)
+    lane_id = lax.broadcasted_iota(jnp.int32, (8, TILE), 1)
+    strips = [block[8 * i : 8 * i + 8, :] for i in range(count)]
+    inverse = [(lane_id == sub_id + 8 * i).astype(jnp.float32) for i in range(count)]
+    for first in range(0, count, group):
+        last = first + group
+        for s in range(first, last):
+            columns = {
+                i: [jnp.broadcast_to(strips[i][:, 8 * s + t : 8 * s + t + 1], (8, TILE)) for t in range(8)]
+                for i in range(s, last)
+            }
+            for t in range(8):
+                lines[s % 2, t] = columns[s][t]
+            lines[s % 2, 8] = strips[s]
+            lines[s % 2, 9] = inverse[s]
+            pivot = {(r, t): spread(lines[s % 2, t, r : r + 1, :]) for t in range(8) for r in range(t, 8)}
+            row = [spread(lines[s % 2, 8, q : q + 1, :]) for q in range(8)]
+            inv_row = [spread(lines[s % 2, 9, q : q + 1, :]) for q in range(8)]
+            for j in range(8):
+                root = lax.rsqrt(pivot[j, j])
+                for r in range(j + 1, 8):
+                    pivot[r, j] = pivot[r, j] * root
+                for t in range(j + 1, 8):
+                    for r in range(t, 8):
+                        pivot[r, t] = pivot[r, t] - pivot[r, j] * pivot[t, j]
+                row[j] = row[j] * root
+                inv_row[j] = inv_row[j] * root
+                for r in range(j + 1, 8):
+                    row[r] = row[r] - pivot[r, j] * row[j]
+                    inv_row[r] = inv_row[r] - pivot[r, j] * inv_row[j]
+                for i in range(s + 1, last):
+                    left = columns[i]
+                    left[j] = left[j] * root
+                    for r in range(j + 1, 8):
+                        left[r] = left[r] - pivot[r, j] * left[j]
+                    strips[i] = strips[i] - left[j] * row[j]
+                    inverse[i] = inverse[i] - left[j] * inv_row[j]
+            for q in range(8):
+                strips[s] = row[q] if q == 0 else jnp.where(sub_id == q, row[q], strips[s])
+                inverse[s] = inv_row[q] if q == 0 else jnp.where(sub_id == q, inv_row[q], inverse[s])
+        if last < count:
+            high, low = split(jnp.concatenate(strips[first:last], axis=0))
+            inv_high, inv_low = split(jnp.concatenate(inverse[first:last], axis=0))
+            three = jnp.concatenate([high, low, high], axis=0)
+            rest = jnp.concatenate([high, high, low], axis=0)
+            inv_rest = jnp.concatenate([inv_high, inv_high, inv_low], axis=0)
+            both = jnp.concatenate([rest, inv_rest], axis=1)
+            change = lax.dot_general(three, both, (((0,), (0,)), ((), ())), preferred_element_type=jnp.float32)
+            for i in range(last, count):
+                strips[i] = strips[i] - change[8 * i : 8 * i + 8, :TILE]
+                inverse[i] = inverse[i] - change[8 * i : 8 * i + 8, TILE:]
+    return jnp.concatenate(inverse, axis=0)
+
+
+def factor_panels(work, u_ref, lines, high, low):
     cols = u_ref.shape[0]
-    work[...] = jnp.zeros_like(work)
-    for p, (i, j) in enumerate(upper_tiles(cols)):
-        work[i : i + TILE, j : j + TILE] = g_ref[p * TILE : (p + 1) * TILE, :]
-    row_id = lax.broadcasted_iota(jnp.int32, (TILE, TILE), 0)
-    lane_id = lax.broadcasted_iota(jnp.int32, (TILE, TILE), 1)
 
     def panel(k, carry):
         base = pl.multiple_of(k * TILE, TILE)
         here = pl.ds(base, TILE)
-        block = work[here, here]
-        strips = [block[i : i + 8, :] for i in range(0, TILE, 8)]
-        unit = (row_id == lane_id).astype(jnp.float32)
-        inverse = [unit[i : i + 8, :] for i in range(0, TILE, 8)]
-        sub_id = lax.broadcasted_iota(jnp.int32, (8, TILE), 0)
-        for j in range(TILE):
-            s, r = divmod(j, 8)
-            row = strips[s][r : r + 1, :]
-            inv_row = inverse[s][r : r + 1, :]
-            root = lax.rsqrt(jnp.broadcast_to(row[:, j : j + 1], (1, TILE)))
-            row = row * root
-            inv_row = inv_row * root
-            for i in range(s, TILE // 8):
-                column = jnp.broadcast_to(strips[i][:, j : j + 1], (8, TILE)) * root
-                if i == s:
-                    column = jnp.where(sub_id > r, column, 0.0)
-                strips[i] = strips[i] - column * row
-                inverse[i] = inverse[i] - column * inv_row
-                if i == s:
-                    inverse[i] = jnp.where(sub_id == r, inv_row, inverse[i])
-        lower_inverse = jnp.concatenate(inverse, axis=0)
-        lower_inverse = jnp.where(lane_id <= row_id, lower_inverse, 0.0)
+        lower = split(factor_block(work[here, here], lines))
         wide_row = lax.broadcasted_iota(jnp.int32, (TILE, cols), 0) + base
         wide_lane = lax.broadcasted_iota(jnp.int32, (TILE, cols), 1)
-        upper = jnp.dot(
-            lower_inverse, work[here, :], precision=exact_mode, preferred_element_type=jnp.float32
+        upper = dot3(lower, split(work[here, :]), ((1,), (0,)))
+        upper = jnp.where(wide_lane >= wide_row, upper, 0.0)
+        u_ref[here, :] = upper
+        high[...], low[...] = split(upper)
+
+        def trail(start, i, inner):
+            there = pl.ds(pl.multiple_of(i * TILE, TILE), TILE)
+            right = (high[:, start:], low[:, start:])
+            work[there, start:] -= dot3((high[:, there], low[:, there]), right, ((0,), (0,)))
+            return inner
+
+        half = cols // TILE // 2
+        lax.fori_loop(k + 1, half, functools.partial(trail, 0), 0)
+        lax.fori_loop(jnp.maximum(k + 1, half), cols // TILE, functools.partial(trail, cols // 2), 0)
+        return carry
+
+    lax.fori_loop(0, cols // TILE, panel, 0)
+
+
+def unpack(source, work, panels):
+    for i, start in enumerate(panel_tiles(panels)[1]):
+        for j in range(i, panels):
+            p = (start + j - i) * TILE
+            work[i * TILE : (i + 1) * TILE, j * TILE : (j + 1) * TILE] = source[p : p + TILE, :]
+
+
+def factor_kernel(g_ref, u_ref, work, lines, high, low):
+    work[...] = jnp.zeros_like(work)
+    unpack(g_ref, work, u_ref.shape[0] // TILE)
+    factor_panels(work, u_ref, lines, high, low)
+
+
+def reduce_factor_kernel(
+    groups, g_ref, u_ref, whole, in1, in2, in3, sum1, sum2, send, arrive, work, lines, high, low
+):
+    pair, plane, line = groups
+    width = lax.axis_size("grp")
+    me = lax.axis_index("rows") * width + lax.axis_index("grp")
+    c, q, b = me % pair, (me // pair) % plane, me // (pair * plane)
+
+    def at(cc, qq, bb):
+        index = (bb * plane + qq) * pair + cc
+        return (index // width, index % width)
+
+    peers = [at((c + t) % pair, q, b) for t in range(1, pair)]
+    peers += [at(c, (q + t) % plane, b) for t in range(1, plane)]
+    peers += [at(c, q, (b + t) % line) for t in range(1, line)]
+    barrier = pltpu.get_barrier_semaphore()
+    for peer in peers:
+        pl.semaphore_signal(barrier, inc=1, device_id=peer, device_id_type=MESH)
+    pl.semaphore_wait(barrier, len(peers))
+
+    runs = segments(u_ref.shape[0] // TILE)
+    copies = {}
+
+    def start(s, stage, t, source, target, peer):
+        slot = stage * 4 + t
+        copy = pltpu.make_async_remote_copy(
+            src_ref=source,
+            dst_ref=target,
+            send_sem=send.at[s, slot],
+            recv_sem=arrive.at[s, slot],
+            device_id=peer,
+            device_id_type=MESH,
         )
-        u_ref[here, :] = jnp.where(wide_lane >= wide_row, upper, 0.0)
-
-        def trail(i, inner):
-            there = pl.ds(pl.multiple_of(i * TILE, TILE), TILE)
-            work[there, :] -= lax.dot_general(
-                u_ref[here, there],
-                u_ref[here, :],
-                (((0,), (0,)), ((), ())),
-                precision=exact_mode,
-                preferred_element_type=jnp.float32,
-            )
-            return inner
-
-        lax.fori_loop(k + 1, cols // TILE, trail, 0)
-        return carry
-
-    lax.fori_loop(0, cols // TILE, panel, 0)
-
-
-def factorize(packed, cols):
-    return pl.pallas_call(
-        factor_kernel,
+        copy.start()
+        copies[s, stage, t] = copy
+
+    def rows(first, count):
+        return pl.ds(pl.multiple_of(first, 8), count)
+
+    def sizes(s):
+        first, tiles = runs[s]
+        first, n1 = first * TILE, tiles * TILE
+        return first, n1 // pair, n1 // (pair * plane), n1 // (pair * plane * line)
+
+    def scatter1(s):
+        first, n1, n2, n3 = sizes(s)
+        for t in range(1, pair):
+            other = (c + t) % pair
+            start(s, 0, t, g_ref.at[rows(first + other * n1, n1)], in1.at[t - 1, rows(first // pair, n1)], at(other, q, b))
+
+    def scatter2(s):
+        first, n1, n2, n3 = sizes(s)
+        mine = rows(first // pair, n1)
+        total = g_ref[rows(first + c * n1, n1), :]
+        for t in range(1, pair):
+            copies[s, 0, t].wait_recv()
+            total = total + in1[t - 1, mine, :]
+        sum1[mine, :] = total
+        for t in range(1, plane):
+            other = (q + t) % plane
+            start(s, 1, t, sum1.at[rows(first // pair + other * n2, n2)], in2.at[t - 1, rows(first // (pair * plane), n2)], at(c, other, b))
+
+    def scatter3(s):
+        first, n1, n2, n3 = sizes(s)
+        mine = rows(first // (pair * plane), n2)
+        total = sum1[rows(first // pair + q * n2, n2), :]
+        for t in range(1, plane):
+            copies[s, 1, t].wait_recv()
+            total = total + in2[t - 1, mine, :]
+        sum2[mine, :] = total
+        for t in range(1, line):
+            other = (b + t) % line
+            start(s, 2, t, sum2.at[rows(first // (pair * plane) + other * n3, n3)], in3.at[t - 1, rows(first // (pair * plane * line), n3)], at(c, q, other))
+
+    def gather3(s):
+        first, n1, n2, n3 = sizes(s)
+        mine = rows(first // (pair * plane * line), n3)
+        total = sum2[rows(first // (pair * plane) + b * n3, n3), :]
+        for t in range(1, line):
+            copies[s, 2, t].wait_recv()
+            total = total + in3[t - 1, mine, :]
+        here = rows(first + c * n1 + q * n2 + b * n3, n3)
+        whole[here, :] = total
+        for t in range(1, line):
+            start(s, 3, t, whole.at[here], whole.at[here], at(c, q, (b + t) % line))
+
+    def gather2(s):
+        first, n1, n2, n3 = sizes(s)
+        for t in range(1, line):
+            copies[s, 3, t].wait_recv()
+        here = rows(first + c * n1 + q * n2, n2)
+        for t in range(1, plane):
+            start(s, 4, t, whole.at[here], whole.at[here], at(c, (q + t) % plane, b))
+
+    def gather1(s):
+        first, n1, n2, n3 = sizes(s)
+        for t in range(1, plane):
+            copies[s, 4, t].wait_recv()
+        here = rows(first + c * n1, n1)
+        for t in range(1, pair):
+            start(s, 5, t, whole.at[here], whole.at[here], at((c + t) % pair, q, b))
+
+    def finish(s):
+        for t in range(1, pair):
+            copies[s, 5, t].wait_recv()
+
+    stages = [scatter1, scatter2, scatter3, gather3, gather2, gather1, finish]
+    for step in range(len(runs) + len(stages) - 1):
+        for k in reversed(range(len(stages))):
+            if 0 <= step - k < len(runs):
+                stages[k](step - k)
+    for copy in copies.values():
+        copy.wait_send()
+    unpack(whole, work, u_ref.shape[0] // TILE)
+    factor_panels(work, u_ref, lines, high, low)
+
+
+def reduce_factor(packed, cols):
+    devices = lax.axis_size("rows") * lax.axis_size("grp")
+    rows = packed.shape[0]
+    common = [
+        pltpu.VMEM((cols, cols), jnp.float32),
+        pltpu.VMEM((2, 10, 8, TILE), jnp.float32),
+        pltpu.VMEM((TILE, cols), jnp.bfloat16),
+        pltpu.VMEM((TILE, cols), jnp.bfloat16),
+    ]
+    call = functools.partial(
+        pl.pallas_call,
         out_shape=jax.ShapeDtypeStruct((cols, cols), jnp.float32),
         in_specs=[pl.BlockSpec(memory_space=pltpu.VMEM)],
         out_specs=pl.BlockSpec(memory_space=pltpu.VMEM),
-        scratch_shapes=[pltpu.VMEM((cols, cols), jnp.float32)],
-        compiler_params=pltpu.CompilerParams(vmem_limit_bytes=VMEM_LIMIT),
+    )
+    pair, plane = 2, 4
+    line = devices // (pair * plane)
+    if devices % (pair * plane) or line > 4 or any(tiles * TILE % (8 * devices) for _, tiles in segments(cols // TILE)):
+        return call(
+            factor_kernel,
+            scratch_shapes=common,
+            compiler_params=pltpu.CompilerParams(vmem_limit_bytes=VMEM_LIMIT),
+        )(lax.psum(packed, ("rows", "grp")))
+    runs = len(segments(cols // TILE))
+    return call(
+        functools.partial(reduce_factor_kernel, (pair, plane, line)),
+        scratch_shapes=[
+            pltpu.VMEM((rows, TILE), jnp.float32),
+            pltpu.VMEM((pair - 1, rows // pair, TILE), jnp.float32),
+            pltpu.VMEM((plane - 1, rows // (pair * plane), TILE), jnp.float32),
+            pltpu.VMEM((max(line - 1, 1), rows // devices, TILE), jnp.float32),
+            pltpu.VMEM((rows // pair, TILE), jnp.float32),
+            pltpu.VMEM((rows // (pair * plane), TILE), jnp.float32),
+            pltpu.SemaphoreType.DMA((runs, 24)),
+            pltpu.SemaphoreType.DMA((runs, 24)),
+            *common,
+        ],
+        compiler_params=pltpu.CompilerParams(vmem_limit_bytes=VMEM_LIMIT, collective_id=1, has_side_effects=True),
     )(packed)
 
 
@@ -215,11 +417,13 @@
     scale = (sample_dev * blocks) ** -0.5
     half = gram_share(arrived, weights, scale)
     whole = (half + half.T) * 0.5
-    packed = jnp.concatenate(
-        [whole[i : i + TILE, j : j + TILE] for i, j in upper_tiles(col_count)], axis=0
-    )
-    summed = lax.psum(packed, ("rows", "grp"))
-    upper_factor = factorize(summed, col_count)
+    pieces = []
+    for i, count in enumerate(panel_tiles(col_count // TILE)[0]):
+        row = whole[i * TILE : (i + 1) * TILE]
+        tiles = [row[:, j * TILE : (j + 1) * TILE] for j in range(i, col_count // TILE)]
+        tiles += [jnp.zeros((TILE, TILE), jnp.float32)] * (count - len(tiles))
+        pieces += tiles
+    upper_factor = reduce_factor(jnp.concatenate(pieces, axis=0), col_count)
     share_rows = col_count // count_rows
     return lax.dynamic_slice_in_dim(
         upper_factor, lax.axis_index("rows") * share_rows, share_rows, 0

time: 537 us -> 362 us (0.67)
  waiting for transfers between devices: 170 us -> 7.71 us
  between operations: 13.7 us -> 0.36 us
    psum x1 -> x0, waiting for transfers between devices: 163 us -> none  [shards(): summed = lax.psum(packed, ('rows', 'grp'))]
  transfers between devices with their start and end apart: 2 -> 1, of which waited for: 2 -> 1; matrix products, arithmetic and copies ran while one was open for 0% -> 0% of each run, Pallas kernels for 0% -> 0%
where the time goes in v1:
time: 362 us
  blocking collectives  177 us (49%)
  Pallas kernels  152 us (42%)
  local copies, waits for them, and re-layouts  11.9 us (3%)
  waiting for transfers between devices  7.71 us (2%)
  starting transfers between devices  7.46 us (2%)
  other arithmetic  5.56 us (2%)
    all_gather x1, blocking collectives, shards(): all_indices = lax.all_gather(samples, ('rows', 'grp'), axis=0)  177 us
    pallas_call x1, Pallas kernels, reduce_factor(): call(functools.partial(reduce_factor_kernel, (pair, plane, line)), scratc...  113 us
    pallas_call x1, Pallas kernels, gram_share(): pl.pallas_call(functools.partial(gram_kernel, scale), grid=(piece // step...  27.5 us
    pallas_call x1, Pallas kernels, local_transform(): pl.pallas_call(functools.partial(local_kernel, base), grid=(cols // TILE,...  11.3 us
    all_to_all x1, waiting for transfers between devices, shards(): lax.all_to_all(before.reshape(blocks, piece_rows, col_count), ('rows', 'g...  7.71 us
    all_to_all x1, starting transfers between devices, shards(): lax.all_to_all(before.reshape(blocks, piece_rows, col_count), ('rows', 'g...  7.46 us
  transfers between devices with their start and end apart: 1, of which 1 were waited for; matrix products, arithmetic and copies ran while one was open for 0% of the time, Pallas kernels for 0%

profile of v1, /device:TPU:0, one launch (start us, length us, event | category | flops | bytes accessed | tf_op | source)
XLA Modules:
  0.0 361.8 jit_solution(8142901366146403286)
XLA Ops:
  0.0 0.7 convert_element_type.7
  0.7 1.3 broadcast_in_dim.4.s_ref
  2.0 11.3 %shard_map.37 = f32[2048,1024]{1,0:T(8,128)} custom-call(f32[2048,1024]{1,0:T(8,128)} %x_ref.1, f32[2048,128]{1,0:T(8,128)} %broadcast_in_dim.4.s_ref, bf16[256,256]{1,0:T(8,128)(2,1)} %constant.49.clone.1.h_ref), custom_call_target="tpu_custom_call" | custom-call | tf_op jit(solution)/shard_map/pallas_call | solution.py:53
  13.3 0.0 copy-start.1
  13.3 7.5 %all-to-all-start = ((f32[32,64,1024]{2,1,0:T(8,128)}), f32[32,64,1024]{2,1,0:T(8,128)}, u32[]{:S(2)}, u32[]{:S(2)}) async-start(f32[32,64,1024]{2,1,0:T(8,128)} %bitcast.8), calls=%async_computation | async-start | bytes 16777216 | tf_op jit(solution)/shard_map/all_to_all | solution.py:405
  20.8 0.0 copy-done.1
  20.8 177.0 %all-gather.1 = s32[32,1,256]{2,1,0:T(1,128)S(1)} all-gather(s32[1,1,256]{2,1,0:T(1,128)S(1)} %bitcast.9), channel_id=2, replica_groups=mesh['rows'=8,'grp'=4] {'rows','grp'}, dimensions={0}, use_global_device_ids=true | all-gather | bytes 33792 | tf_op jit(solution)/shard_map/all_gather | solution.py:402
  197.8 0.1 bitcast_subtract_fusion
  197.9 0.3 convert_reduce_fusion
  198.3 7.7 %all-to-all-done.x_ref = f32[32,64,1024]{2,1,0:T(8,128)} async-done(((f32[32,64,1024]{2,1,0:T(8,128)}), f32[32,64,1024]{2,1,0:T(8,128)}, u32[]{:S(2)}, u32[]{:S(2)}) %all-to-all-start) | async-done | bytes 8388640 | tf_op jit(solution)/shard_map/all_to_all | solution.py:405
  206.0 1.4 broadcast_in_dim.5.w_ref
  207.3 27.5 %shard_map.38 = f32[1024,1024]{1,0:T(8,128)} custom-call(f32[32,64,1024]{2,1,0:T(8,128)} %all-to-all-done.x_ref, f32[32,64,128]{2,1,0:T(8,128)} %broadcast_in_dim.5.w_ref), custom_call_target="tpu_custom_call" | custom-call | tf_op jit(solution)/shard_map/pallas_call | solution.py:107
  234.9 5.3 %copy.6 = f32[1024,1024]{0,1:T(8,128)} copy(f32[1024,1024]{1,0:T(8,128)} %shard_map.38) | data formatting | bytes 8388608 | tf_op jit(solution)/shard_map/pallas_call | solution.py:107
  240.2 4.4 %fusion = f32[1024,1024]{1,0:T(8,128)S(1)} fusion(f32[1024,1024]{1,0:T(8,128)} %shard_map.38, f32[1024,1024]{0,1:T(8,128)} %copy.6), kind=kLoop, calls=%fused_computation.1 | loop fusion | flops 2097152 | bytes 12582912 | tf_op jit(solution)/shard_map/mul | solution.py:419
  245.4 0.0 copy-start
  245.4 1.5 copy-done
  246.9 113.0 %shard_map.39 = f32[1024,1024]{1,0:T(8,128)} custom-call(f32[5120,128]{1,0:T(8,128)} %copy-done), custom_call_target="tpu_custom_call" | custom-call | tf_op jit(solution)/shard_map/pallas_call | solution.py:378
  359.9 1.9 constant_dynamic-slice_fusion
  (40 shorter events, 0.4 us)
Async XLA Ops:
  13.3 7.5 %copy-start.1 = (s32[256]{0:T(256)S(1)}, s32[256]{0:T(256)}, u32[]{:S(2)}) copy-start(s32[256]{0:T(256)} %param.5) | copy-start | bytes 3076
  13.3 192.6 %all-to-all-start = ((f32[32,64,1024]{2,1,0:T(8,128)}), f32[32,64,1024]{2,1,0:T(8,128)}, u32[]{:S(2)}, u32[]{:S(2)}) async-start(f32[32,64,1024]{2,1,0:T(8,128)} %bitcast.8), calls=%async_computation | async-start | bytes 16777216 | tf_op jit(solution)/shard_map/all_to_all | solution.py:405
  245.4 1.5 copy-start

commit v2 on v1

--- a/solution.py
+++ b/solution.py
@@ -228,14 +228,15 @@
             work[i * TILE : (i + 1) * TILE, j * TILE : (j + 1) * TILE] = source[p : p + TILE, :]
 
 
-def factor_kernel(g_ref, u_ref, work, lines, high, low):
+def factor_kernel(g_ref, u_ref, over_ref, work, lines, high, low):
+    over_ref[...] = g_ref[g_ref.shape[0] - 8 :, :]
     work[...] = jnp.zeros_like(work)
     unpack(g_ref, work, u_ref.shape[0] // TILE)
     factor_panels(work, u_ref, lines, high, low)
 
 
 def reduce_factor_kernel(
-    groups, g_ref, u_ref, whole, in1, in2, in3, sum1, sum2, send, arrive, work, lines, high, low
+    groups, g_ref, u_ref, over_ref, whole, in1, in2, in3, sum1, sum2, send, arrive, work, lines, high, low
 ):
     pair, plane, line = groups
     width = lax.axis_size("grp")
@@ -347,6 +348,7 @@
                 stages[k](step - k)
     for copy in copies.values():
         copy.wait_send()
+    over_ref[...] = whole[whole.shape[0] - 8 :, :]
     unpack(whole, work, u_ref.shape[0] // TILE)
     factor_panels(work, u_ref, lines, high, low)
 
@@ -362,9 +364,9 @@
     ]
     call = functools.partial(
         pl.pallas_call,
-        out_shape=jax.ShapeDtypeStruct((cols, cols), jnp.float32),
+        out_shape=[jax.ShapeDtypeStruct((cols, cols), jnp.float32), jax.ShapeDtypeStruct((8, TILE), jnp.float32)],
         in_specs=[pl.BlockSpec(memory_space=pltpu.VMEM)],
-        out_specs=pl.BlockSpec(memory_space=pltpu.VMEM),
+        out_specs=[pl.BlockSpec(memory_space=pltpu.VMEM)] * 2,
     )
     pair, plane = 2, 4
     line = devices // (pair * plane)
@@ -392,14 +394,203 @@
     )(packed)
 
 
-def shards(matrix, row_signs, samples):
-    count_rows = lax.axis_size("rows")
-    blocks = count_rows * lax.axis_size("grp")
+def exchange_kernel(
+    sizes, scale, x_ref, s_ref, h_ref, pick_ref, w_ref, over_ref, g_ref,
+    x_in, signed_h, x_out, x_got, mixed, y_out, y_got, high, low, load, send_a, got_a, send_b, got_b,
+):
+    near, far, ahead = sizes
+    steps, rows = x_in.shape[0], x_in.shape[1]
+    base, piece, share = h_ref.shape[0], rows // near, pick_ref.shape[0] // far
+    width = lax.axis_size("grp")
+    me = lax.axis_index("rows") * width + lax.axis_index("grp")
+    a, b = me % near, me // near
+
+    def at(aa, bb):
+        index = bb * near + aa
+        return (index // width, index % width)
+
+    def loading(c):
+        lanes = pl.ds(pl.multiple_of(c * TILE, TILE), TILE)
+        return pltpu.make_async_copy(x_ref.at[:, lanes], x_in.at[c], load.at[c])
+
+    def span(i, count):
+        return pl.ds(pl.multiple_of(i * count, count), count)
+
+    def near_copy(c, t):
+        there = (a + t) % near
+        return pltpu.make_async_remote_copy(
+            src_ref=x_out.at[c, span(there, piece)],
+            dst_ref=x_got.at[c, span(a, piece)],
+            send_sem=send_a.at[c, t],
+            recv_sem=got_a.at[c, t],
+            device_id=at(there, b),
+            device_id_type=MESH,
+        )
+
+    def far_copy(c, t):
+        there = (b + t) % far
+        return pltpu.make_async_remote_copy(
+            src_ref=y_out.at[c, span(there, share)],
+            dst_ref=y_got.at[c, span(b, share)],
+            send_sem=send_b.at[c, t],
+            recv_sem=got_b.at[c, t],
+            device_id=at(a, there),
+            device_id_type=MESH,
+        )
+
+    def each(first, last, act):
+        def body(t, carry):
+            act(t)
+            return carry
+
+        lax.fori_loop(first, last, body, 0)
+
+    def transform(c):
+        loading(c).wait()
+        parts = []
+        for i in range(rows // base):
+            x_high, x_low = split(x_in[c, i * base : (i + 1) * base, :])
+            part = jnp.dot(signed_h[i], x_high, preferred_element_type=jnp.float32)
+            parts.append(part + jnp.dot(signed_h[i], x_low, preferred_element_type=jnp.float32))
+        for i, part in enumerate(butterfly(parts)):
+            x_out[c, i * base : (i + 1) * base, :] = part
+        each(1, near, lambda t: near_copy(c, t).start())
+        x_got[c, span(a, piece), :] = x_out[c, span(a, piece), :]
+
+    def middle(c):
+        each(1, near, lambda t: near_copy(c, t).wait_recv())
+        block = min(32, piece)
+
+        def mix(r):
+            where = [pl.ds(pl.multiple_of(j * piece + r * block, block), block) for j in range(near)]
+            for here, part in zip(where, butterfly([x_got[c, here, :] for here in where])):
+                mixed[here, :] = part
+
+        each(0, piece // block, mix)
+
+        def keep(r):
+            for u in range(8):
+                y_out[c, pl.ds(pl.multiple_of(r * 8, 8) + u, 1), :] = mixed[pl.ds(pick_ref[r * 8 + u], 1), :]
+
+        each(0, pick_ref.shape[0] // 8, keep)
+        each(1, far, lambda t: far_copy(c, t).start())
+        y_got[c, span(b, share), :] = y_out[c, span(b, share), :]
+
+    def last(c):
+        each(1, far, lambda t: far_copy(c, t).wait_recv())
+        lanes = pl.ds(pl.multiple_of(c * TILE, TILE), TILE)
+
+        def mix(r):
+            where = [pl.ds(pl.multiple_of(j * share + r * 16, 16), 16) for j in range(far)]
+            for here, part in zip(where, butterfly([y_got[c, here, :] for here in where])):
+                x_high, x_low = split(part * (w_ref[here, :] * scale))
+                high[here, lanes] = x_high
+                low[here, lanes] = x_low
+
+        each(0, share // 16, mix)
+
+        def gram(i):
+            left = pl.ds(pl.multiple_of(i * TILE, TILE), TILE)
+            half = i // 2
+            first = 2 * steps * half - 2 * half * (half - 1) + (i % 2) * (steps - 2 * half)
+            tile = dot3((high[:, left], low[:, left]), (high[:, lanes], low[:, lanes]), ((0,), (0,)))
+            g_ref[span(first + c - i, TILE), :] = tile
+
+        each(0, c + 1, gram)
+
+    each(0, steps, lambda c: loading(c).start())
+    barrier = pltpu.get_barrier_semaphore()
+
+    def greet(there):
+        pl.semaphore_signal(barrier, inc=1, device_id=there, device_id_type=MESH)
+
+    each(1, near, lambda t: greet(at((a + t) % near, b)))
+    each(1, far, lambda t: greet(at(a, (b + t) % far)))
+    for i in range(rows // base):
+        signed_h[i] = (h_ref[...] * s_ref[i : i + 1, :]).astype(jnp.bfloat16)
+    sizes_list, starts = panel_tiles(steps)
+    for i in range(1, steps, 2):
+        spare = (starts[i] + sizes_list[i] - 1) * TILE
+        g_ref[spare : spare + TILE, :] = jnp.zeros((TILE, TILE), jnp.float32)
+    g_ref[g_ref.shape[0] - 8 :, :] = over_ref[...]
+    pl.semaphore_wait(barrier, near + far - 2)
+    each(0, ahead, transform)
+
+    def step(c):
+        @pl.when(c + ahead < steps)
+        def _():
+            transform(c + ahead)
+
+        middle(c)
+
+        @pl.when(c > 0)
+        def _():
+            last(c - 1)
+
+    each(0, steps, step)
+    last(steps - 1)
+    each(0, steps, lambda c: each(1, near, lambda t: near_copy(c, t).wait_send()))
+    each(0, steps, lambda c: each(1, far, lambda t: far_copy(c, t).wait_send()))
+
+
+def exchange(matrix, row_signs, all_indices, near, far, room, scale):
+    rows, cols = matrix.shape
+    steps, piece, share = cols // TILE, rows // near, room // far
+    base = min(256, rows)
+    width = lax.axis_size("grp")
+    me = lax.axis_index("rows") * width + lax.axis_index("grp")
+    a, b = me % near, me // near
+    blocks = near * far
+    within = all_indices - (jnp.arange(blocks, dtype=jnp.int32)[:, None] * rows + a * piece)
+    hits = within[:, None, :] == jnp.arange(piece, dtype=jnp.int32)[None, :, None]
+    taken = jnp.max(hits.astype(jnp.float32), axis=2).reshape(far, rows)
+    needed = jnp.max(taken, axis=0).reshape(rows // TILE, TILE)
+    lane = jnp.arange(TILE)
+    before = jnp.dot(needed, (lane[:, None] < lane[None, :]).astype(jnp.float32), preferred_element_type=jnp.float32)
+    line_sum = jnp.sum(needed, axis=1)
+    line = jnp.arange(rows // TILE)
+    before = before + jnp.sum(jnp.where(line[None, :] < line[:, None], line_sum[None, :], 0.0), axis=1)[:, None]
+    slot = jnp.where(needed > 0, before, -1.0).reshape(rows).astype(jnp.int32)
+    hot = jnp.arange(room, dtype=jnp.int32)[:, None] == slot[None, :]
+    row = jnp.arange(rows, dtype=jnp.int32)
+    pick = jnp.sum(jnp.where(hot, row[None, :], 0), axis=1)
+    mine = lax.dynamic_slice_in_dim(hot, b * share, share, 0)
+    weights = jnp.max(jnp.where(mine[None, :, :], taken[:, None, :], 0.0), axis=2)
+    weights = jnp.broadcast_to(weights.reshape(room, 1), (room, TILE))
+    over = (jnp.sum(line_sum) > room).astype(jnp.float32)
+    over = jnp.broadcast_to(over, (8, TILE))
+    tiles = sum(panel_tiles(steps)[0])
+    vmem = pl.BlockSpec(memory_space=pltpu.VMEM)
+    return pl.pallas_call(
+        functools.partial(exchange_kernel, (near, far, min(3, steps)), scale),
+        out_shape=jax.ShapeDtypeStruct((tiles * TILE, TILE), jnp.float32),
+        in_specs=[pl.BlockSpec(memory_space=pl.ANY), vmem, vmem, pl.BlockSpec(memory_space=pltpu.SMEM), vmem, vmem],
+        out_specs=vmem,
+        scratch_shapes=[
+            pltpu.VMEM((steps, rows, TILE), jnp.float32),
+            pltpu.VMEM((rows // base, base, base), jnp.bfloat16),
+            pltpu.VMEM((steps, rows, TILE), jnp.float32),
+            pltpu.VMEM((steps, rows, TILE), jnp.float32),
+            pltpu.VMEM((rows, TILE), jnp.float32),
+            pltpu.VMEM((steps, room, TILE), jnp.float32),
+            pltpu.VMEM((steps, room, TILE), jnp.float32),
+            pltpu.VMEM((room, cols), jnp.bfloat16),
+            pltpu.VMEM((room, cols), jnp.bfloat16),
+            pltpu.SemaphoreType.DMA((steps,)),
+            pltpu.SemaphoreType.DMA((steps, near)),
+            pltpu.SemaphoreType.DMA((steps, near)),
+            pltpu.SemaphoreType.DMA((steps, far)),
+            pltpu.SemaphoreType.DMA((steps, far)),
+        ],
+        compiler_params=pltpu.CompilerParams(vmem_limit_bytes=VMEM_LIMIT, collective_id=2, has_side_effects=True),
+    )(matrix, row_signs.astype(jnp.float32).reshape(rows // base, base), sylvester(base), pick, weights, over)
+
+
+def whole_exchange(matrix, row_signs, all_indices, scale):
+    blocks = lax.axis_size("rows") * lax.axis_size("grp")
     row_dev, col_count = matrix.shape
     piece_rows = row_dev // blocks
-    sample_dev = samples.shape[0]
     position = lax.axis_index(("rows", "grp"))
-    all_indices = lax.all_gather(samples, ("rows", "grp"), axis=0)
     signs = jnp.broadcast_to(row_signs.astype(jnp.float32)[:, None], (row_dev, TILE))
     before = local_transform(matrix, signs, min(256, row_dev))
     arrived = lax.all_to_all(
@@ -414,7 +605,6 @@
     hits = within[:, None, :] == jnp.arange(piece_rows, dtype=jnp.int32)[None, :, None]
     weights = jnp.max(hits.astype(jnp.float32), axis=2)
     weights = jnp.broadcast_to(weights[:, :, None], (blocks, piece_rows, TILE))
-    scale = (sample_dev * blocks) ** -0.5
     half = gram_share(arrived, weights, scale)
     whole = (half + half.T) * 0.5
     pieces = []
@@ -423,11 +613,34 @@
         tiles = [row[:, j * TILE : (j + 1) * TILE] for j in range(i, col_count // TILE)]
         tiles += [jnp.zeros((TILE, TILE), jnp.float32)] * (count - len(tiles))
         pieces += tiles
-    upper_factor = reduce_factor(jnp.concatenate(pieces, axis=0), col_count)
+    return jnp.concatenate(pieces, axis=0)
+
+
+def shards(matrix, row_signs, samples):
+    count_rows = lax.axis_size("rows")
+    blocks = count_rows * lax.axis_size("grp")
+    row_dev, col_count = matrix.shape
+    sample_dev = samples.shape[0]
+    scale = (sample_dev * blocks) ** -0.5
+    all_indices = lax.all_gather(samples, ("rows", "grp"), axis=0)
+    far = 4
+    near = blocks // far
+    chance = 1.0 - (1.0 - sample_dev / row_dev) ** far
+    room = row_dev * chance + 5.0 * (row_dev * chance * (1.0 - chance)) ** 0.5
+    room = min(row_dev, -(-int(room) // (16 * far)) * 16 * far)
     share_rows = col_count // count_rows
-    return lax.dynamic_slice_in_dim(
-        upper_factor, lax.axis_index("rows") * share_rows, share_rows, 0
-    )
+
+    def own(upper_factor):
+        return lax.dynamic_slice_in_dim(upper_factor, lax.axis_index("rows") * share_rows, share_rows, 0)
+
+    packed = exchange(matrix, row_signs, all_indices, near, far, room, scale)
+    upper_factor, over = reduce_factor(packed, col_count)
+
+    def again():
+        packed = whole_exchange(matrix, row_signs, all_indices, scale)
+        return own(reduce_factor(packed, col_count)[0])
+
+    return lax.cond(over[0, 0] > 0.0, again, lambda: own(upper_factor))
 
 
 def solution(mesh):

time: 362 us -> 258 us (0.71)
  blocking collectives: 177 us -> 43.6 us
  Pallas kernels: 152 us -> 200 us
  waiting for transfers between devices: 7.71 us -> 0 us
  starting transfers between devices: 7.46 us -> 0 us
  local copies, waits for them, and re-layouts: 11.9 us -> 5.38 us
    all_gather x1, blocking collectives: 177 us -> 43.6 us  [shards(): all_indices = lax.all_gather(samples, ('rows', 'grp'), axis=0)]
    pallas_call x2 -> x1, Pallas kernels: 38.9 us -> 108 us  [exchange(): pl.pallas_call(functools.partial(exchange_kernel, (near, far, min(3, step...]
    pallas_call x1, Pallas kernels: 113 us -> 92.1 us  [reduce_factor(): call(functools.partial(reduce_factor_kernel, (pair, plane, line)), scratc...]
    all_to_all x1 -> x0, waiting for transfers between devices: 7.71 us -> none  [shards(): lax.all_to_all(before.reshape(blocks, piece_rows, col_count), ('rows', 'g...]
    all_to_all x1 -> x0, starting transfers between devices: 7.46 us -> none  [shards(): lax.all_to_all(before.reshape(blocks, piece_rows, col_count), ('rows', 'g...]
    pallas_call x1 -> x0, local copies, waits for them, and re-layouts: 5.35 us -> none  [gram_share(): pl.pallas_call(functools.partial(gram_kernel, scale), grid=(piece // step...]
    mul x1 -> x0, other arithmetic: 4.43 us -> none  [shards(): whole = (half + half.T) * 0.5]
  transfers between devices with their start and end apart: 1 -> 0, of which waited for: 1 -> 0; matrix products, arithmetic and copies ran while one was open for 0% -> 0% of each run, Pallas kernels for 0% -> 0%
where the time goes in v2:
time: 258 us
  Pallas kernels  200 us (78%)
  blocking collectives  43.6 us (17%)
  other arithmetic  7.12 us (3%)
  local copies, waits for them, and re-layouts  5.38 us (2%)
    pallas_call x1, Pallas kernels, exchange(): pl.pallas_call(functools.partial(exchange_kernel, (near, far, min(3, step...  108 us
    pallas_call x1, Pallas kernels, reduce_factor(): call(functools.partial(reduce_factor_kernel, (pair, plane, line)), scratc...  92.1 us
    all_gather x1, blocking collectives, shards(): all_indices = lax.all_gather(samples, ('rows', 'grp'), axis=0)  43.6 us

profile of v2, /device:TPU:0, one launch (start us, length us, event | category | flops | bytes accessed | tf_op | source)
XLA Modules:
  0.0 257.9 jit_solution(1362327753856002318)
XLA Ops:
  0.0 0.7 convert_element_type.33
  0.7 0.6 reshape.47.s_ref
  1.3 43.6 %all-gather.1 = s32[32,1,256]{2,1,0:T(1,128)S(1)} all-gather(s32[1,1,256]{2,1,0:T(1,128)} %bitcast.23), channel_id=2, replica_groups=mesh['rows'=8,'grp'=4] {'rows','grp'}, dimensions={0}, use_global_device_ids=true | all-gather | bytes 33792 | tf_op jit(solution)/shard_map/all_gather | solution.py:625
  44.9 0.1 broadcast_subtract_fusion.1
  44.9 1.2 convert_reduce_fusion.1
  46.2 0.1 bitcast_reduce_fusion
  46.3 0.1 select_reduce_fusion.2
  46.4 0.1 fusion.3
  46.5 1.5 select_reduce_fusion.1.pick_ref
  48.1 1.5 iota_compare_fusion.2
  49.7 1.2 select_reduce_fusion
  50.8 0.1 broadcast_in_dim.94
  50.9 1.0 broadcast_in_dim.95.w_ref
  51.9 0.7 reduce_sum.39
  53.2 0.6 broadcast_in_dim.96.over_ref
  53.8 108.2 %shard_map.39.g_ref = f32[5120,128]{1,0:T(8,128)} custom-call(f32[2048,1024]{1,0:T(8,128)} %x_ref.1, f32[8,256]{1,0:T(8,128)} %reshape.47.s_ref, f32[256,256]{1,0:T(8,128)} %constant.145.clone.1.h_ref, s32[960]{0:T(1024)} %select_reduce_fusion.1.pick_ref, f32[960,128]{1,0:T(8,128)} %broadcast_in_dim.95.w_ref, f32[8,128]{1,0:T(8,128)} %broadcast_in_dim.96.over_ref), custom_call_target="tpu_custom_call" | custom-call | tf_op jit(solution)/shard_map/pallas_call | solution.py:564
  162.0 0.0 copy-start.2
  162.0 92.1 %shard_map.40 = (f32[1024,1024]{1,0:T(8,128)}, f32[8,128]{1,0:T(8,128)}) custom-call(f32[5120,128]{1,0:T(8,128)} %shard_map.39.g_ref), custom_call_target="tpu_custom_call" | custom-call | tf_op jit(solution)/shard_map/pallas_call | solution.py:380
  254.1 1.2 slice.154
  255.9 0.0 copy-done.2
  255.9 1.1 conditional.1
  256.0 1.1 constant_dynamic-slice_fusion
  257.1 0.0 copy-start.1
  257.1 0.8 copy-done.1
  (5 shorter events, 0.1 us)
Async XLA Ops:
  162.0 93.9 %copy-start.2 = (s32[2048]{0:T(1024)S(1)}, s32[2048]{0:T(1024)}, u32[]{:S(2)}) copy-start(s32[2048]{0:T(1024)} %param.6) | copy-start | bytes 24580
  257.1 0.8 copy-start.1

commit v3 on v2

--- a/solution.py
+++ b/solution.py
@@ -395,12 +395,14 @@
 
 
 def exchange_kernel(
-    sizes, scale, x_ref, s_ref, h_ref, pick_ref, w_ref, over_ref, g_ref,
-    x_in, signed_h, x_out, x_got, mixed, y_out, y_got, high, low, load, send_a, got_a, send_b, got_b,
+    sizes, scale, x_ref, s_ref, h_ref, samples_ref, g_ref,
+    x_in, signed_h, x_out, x_got, mixed, y_out, y_got, high, low, samples, taken, weights, pick_row, pick_ref,
+    load, send_a, got_a, send_b, got_b, send_s, got_s,
 ):
     near, far, ahead = sizes
     steps, rows = x_in.shape[0], x_in.shape[1]
-    base, piece, share = h_ref.shape[0], rows // near, pick_ref.shape[0] // far
+    base, piece, share = h_ref.shape[0], rows // near, weights.shape[0] // far
+    room = share * far
     width = lax.axis_size("grp")
     me = lax.axis_index("rows") * width + lax.axis_index("grp")
     a, b = me % near, me // near
@@ -444,6 +446,83 @@
             return carry
 
         lax.fori_loop(first, last, body, 0)
+
+    def picked(group, offset):
+        return jnp.minimum(jnp.maximum(pick_ref[group, offset], 0), rows - 1)
+
+    def sample_copy(t, along):
+        there = at((a + t) % near, b) if along == 0 else at(a, (b + t) % far)
+        source = samples_ref if along == 0 else samples.at[pl.ds(b * near, near)]
+        target = samples.at[me] if along == 0 else samples.at[pl.ds(b * near, near)]
+        return pltpu.make_async_remote_copy(
+            src_ref=source,
+            dst_ref=target,
+            send_sem=send_s.at[along * near + t],
+            recv_sem=got_s.at[along * near + t],
+            device_id=there,
+            device_id_type=MESH,
+        )
+
+    def choose():
+        lines = samples_ref.shape[0]
+        position = lax.broadcasted_iota(jnp.int32, (piece, TILE), 0)
+        ones = jnp.ones((TILE, TILE), jnp.bfloat16)
+
+        def presence(kl):
+            where = pl.ds(pl.multiple_of(kl * piece, piece), piece)
+            for kz in range(far):
+                block = kz * near + kl
+                hits = jnp.zeros((piece, TILE), jnp.float32)
+                for i in range(lines):
+                    within = samples[block, i : i + 1, :] - (block * rows + a * piece)
+                    hits += jnp.where(position == within, 1.0, 0.0)
+                taken[kz, where, :] = jnp.dot(hits.astype(jnp.bfloat16), ones, preferred_element_type=jnp.float32)
+
+        each(0, near, presence)
+        row_id = lax.broadcasted_iota(jnp.int32, (TILE, TILE), 0)
+        lane_id = lax.broadcasted_iota(jnp.int32, (TILE, TILE), 1)
+        earlier = jnp.where(lane_id < row_id, 1.0, 0.0).astype(jnp.bfloat16)
+        total = jnp.zeros((1, TILE), jnp.float32)
+        for i in range(rows // TILE):
+            here = slice(i * TILE, (i + 1) * TILE)
+            need = taken[0, here, :]
+            for kz in range(1, far):
+                need = jnp.maximum(need, taken[kz, here, :])
+            rank = jnp.dot(earlier, need.astype(jnp.bfloat16), preferred_element_type=jnp.float32)
+            mixed[here, :] = jnp.where(need > 0.0, rank + total, -1.0)
+            total = total + rank[TILE - 1 :, :] + need[TILE - 1 :, :]
+        lane = lax.broadcasted_iota(jnp.int32, (8, TILE), 1).astype(jnp.float32)
+        sub = lax.broadcasted_iota(jnp.int32, (8, TILE), 0).astype(jnp.float32)
+        tiles = pick_row.shape[0]
+
+        def find(r, found):
+            for u in range(4):
+                slot = mixed[pl.ds(pl.multiple_of(r * 32 + u * 8, 8), 8), :]
+                number = sub + (r * 32 + u * 8).astype(jnp.float32)
+                found = tuple(f + jnp.where(slot == lane + float(v * TILE), number, 0.0) for v, f in enumerate(found))
+            return found
+
+        found = lax.fori_loop(0, rows // 32, find, (jnp.zeros((8, TILE), jnp.float32),) * tiles)
+        for v in range(tiles):
+            pick_row[v : v + 1, :] = jnp.sum(found[v], axis=0, keepdims=True).astype(jnp.int32)
+        copy = pltpu.make_async_copy(pick_row, pick_ref, load.at[steps])
+        copy.start()
+        copy.wait()
+
+        def weigh(r):
+            for u in range(8):
+                place = b * share + r * 8 + u
+                row = picked(place // TILE, place % TILE)
+                for kz in range(far):
+                    weights[pl.ds(pl.multiple_of(kz * share + r * 8, 8) + u, 1), :] = taken[kz, pl.ds(row, 1), :]
+
+        each(0, share // 8, weigh)
+        slot = lax.broadcasted_iota(jnp.int32, (share, TILE), 0) + b * share
+        used = jnp.where(slot.astype(jnp.float32) < total, scale, 0.0)
+        for kz in range(far):
+            here = slice(kz * share, (kz + 1) * share)
+            weights[here, :] = weights[here, :] * used
+        g_ref[g_ref.shape[0] - 8 :, :] = jnp.broadcast_to(jnp.where(total > float(room), 1.0, 0.0), (8, TILE))
 
     def transform(c):
         loading(c).wait()
@@ -469,10 +548,12 @@
         each(0, piece // block, mix)
 
         def keep(r):
-            for u in range(8):
-                y_out[c, pl.ds(pl.multiple_of(r * 8, 8) + u, 1), :] = mixed[pl.ds(pick_ref[r * 8 + u], 1), :]
-
-        each(0, pick_ref.shape[0] // 8, keep)
+            group, offset = (r * 32) // TILE, (r * 32) % TILE
+            kept = [mixed[pl.ds(picked(group, offset + u), 1), :] for u in range(32)]
+            for u in range(0, 32, 8):
+                y_out[c, pl.ds(pl.multiple_of(r * 32 + u, 8), 8), :] = jnp.concatenate(kept[u : u + 8], axis=0)
+
+        each(0, room // 32, keep)
         each(1, far, lambda t: far_copy(c, t).start())
         y_got[c, span(b, share), :] = y_out[c, span(b, share), :]
 
@@ -483,7 +564,7 @@
         def mix(r):
             where = [pl.ds(pl.multiple_of(j * share + r * 16, 16), 16) for j in range(far)]
             for here, part in zip(where, butterfly([y_got[c, here, :] for here in where])):
-                x_high, x_low = split(part * (w_ref[here, :] * scale))
+                x_high, x_low = split(part * weights[here, :])
                 high[here, lanes] = x_high
                 low[here, lanes] = x_low
 
@@ -512,9 +593,15 @@
     for i in range(1, steps, 2):
         spare = (starts[i] + sizes_list[i] - 1) * TILE
         g_ref[spare : spare + TILE, :] = jnp.zeros((TILE, TILE), jnp.float32)
-    g_ref[g_ref.shape[0] - 8 :, :] = over_ref[...]
+    samples[me] = samples_ref[...]
     pl.semaphore_wait(barrier, near + far - 2)
-    each(0, ahead, transform)
+    each(1, near, lambda t: sample_copy(t, 0).start())
+    transform(0)
+    each(1, near, lambda t: sample_copy(t, 0).wait_recv())
+    each(1, far, lambda t: sample_copy(t, 1).start())
+    each(1, ahead, transform)
+    each(1, far, lambda t: sample_copy(t, 1).wait_recv())
+    choose()
 
     def step(c):
         @pl.when(c + ahead < steps)
@@ -529,42 +616,25 @@
 
     each(0, steps, step)
     last(steps - 1)
+    each(1, near, lambda t: sample_copy(t, 0).wait_send())
+    each(1, far, lambda t: sample_copy(t, 1).wait_send())
     each(0, steps, lambda c: each(1, near, lambda t: near_copy(c, t).wait_send()))
     each(0, steps, lambda c: each(1, far, lambda t: far_copy(c, t).wait_send()))
 
 
-def exchange(matrix, row_signs, all_indices, near, far, room, scale):
+def exchange(matrix, row_signs, samples, near, far, room, scale):
     rows, cols = matrix.shape
-    steps, piece, share = cols // TILE, rows // near, room // far
+    steps = cols // TILE
     base = min(256, rows)
-    width = lax.axis_size("grp")
-    me = lax.axis_index("rows") * width + lax.axis_index("grp")
-    a, b = me % near, me // near
-    blocks = near * far
-    within = all_indices - (jnp.arange(blocks, dtype=jnp.int32)[:, None] * rows + a * piece)
-    hits = within[:, None, :] == jnp.arange(piece, dtype=jnp.int32)[None, :, None]
-    taken = jnp.max(hits.astype(jnp.float32), axis=2).reshape(far, rows)
-    needed = jnp.max(taken, axis=0).reshape(rows // TILE, TILE)
-    lane = jnp.arange(TILE)
-    before = jnp.dot(needed, (lane[:, None] < lane[None, :]).astype(jnp.float32), preferred_element_type=jnp.float32)
-    line_sum = jnp.sum(needed, axis=1)
-    line = jnp.arange(rows // TILE)
-    before = before + jnp.sum(jnp.where(line[None, :] < line[:, None], line_sum[None, :], 0.0), axis=1)[:, None]
-    slot = jnp.where(needed > 0, before, -1.0).reshape(rows).astype(jnp.int32)
-    hot = jnp.arange(room, dtype=jnp.int32)[:, None] == slot[None, :]
-    row = jnp.arange(rows, dtype=jnp.int32)
-    pick = jnp.sum(jnp.where(hot, row[None, :], 0), axis=1)
-    mine = lax.dynamic_slice_in_dim(hot, b * share, share, 0)
-    weights = jnp.max(jnp.where(mine[None, :, :], taken[:, None, :], 0.0), axis=2)
-    weights = jnp.broadcast_to(weights.reshape(room, 1), (room, TILE))
-    over = (jnp.sum(line_sum) > room).astype(jnp.float32)
-    over = jnp.broadcast_to(over, (8, TILE))
+    lines = -(-samples.shape[0] // TILE)
+    padded = jnp.pad(samples, (0, lines * TILE - samples.shape[0]), constant_values=-1).reshape(lines, TILE)
     tiles = sum(panel_tiles(steps)[0])
     vmem = pl.BlockSpec(memory_space=pltpu.VMEM)
+    picks = -(-room // TILE)
     return pl.pallas_call(
         functools.partial(exchange_kernel, (near, far, min(3, steps)), scale),
         out_shape=jax.ShapeDtypeStruct((tiles * TILE, TILE), jnp.float32),
-        in_specs=[pl.BlockSpec(memory_space=pl.ANY), vmem, vmem, pl.BlockSpec(memory_space=pltpu.SMEM), vmem, vmem],
+        in_specs=[pl.BlockSpec(memory_space=pl.ANY), vmem, vmem, vmem],
         out_specs=vmem,
         scratch_shapes=[
             pltpu.VMEM((steps, rows, TILE), jnp.float32),
@@ -576,14 +646,21 @@
             pltpu.VMEM((steps, room, TILE), jnp.float32),
             pltpu.VMEM((room, cols), jnp.bfloat16),
             pltpu.VMEM((room, cols), jnp.bfloat16),
-            pltpu.SemaphoreType.DMA((steps,)),
+            pltpu.VMEM((near * far, lines, TILE), jnp.int32),
+            pltpu.VMEM((far, rows, TILE), jnp.float32),
+            pltpu.VMEM((room, TILE), jnp.float32),
+            pltpu.VMEM((picks, TILE), jnp.int32),
+            pltpu.SMEM((picks, TILE), jnp.int32),
+            pltpu.SemaphoreType.DMA((steps + 1,)),
             pltpu.SemaphoreType.DMA((steps, near)),
             pltpu.SemaphoreType.DMA((steps, near)),
             pltpu.SemaphoreType.DMA((steps, far)),
             pltpu.SemaphoreType.DMA((steps, far)),
+            pltpu.SemaphoreType.DMA((near + far,)),
+            pltpu.SemaphoreType.DMA((near + far,)),
         ],
         compiler_params=pltpu.CompilerParams(vmem_limit_bytes=VMEM_LIMIT, collective_id=2, has_side_effects=True),
-    )(matrix, row_signs.astype(jnp.float32).reshape(rows // base, base), sylvester(base), pick, weights, over)
+    )(matrix, row_signs.astype(jnp.float32).reshape(rows // base, base), sylvester(base), padded)
 
 
 def whole_exchange(matrix, row_signs, all_indices, scale):
@@ -622,7 +699,6 @@
     row_dev, col_count = matrix.shape
     sample_dev = samples.shape[0]
     scale = (sample_dev * blocks) ** -0.5
-    all_indices = lax.all_gather(samples, ("rows", "grp"), axis=0)
     far = 4
     near = blocks // far
     chance = 1.0 - (1.0 - sample_dev / row_dev) ** far
@@ -633,10 +709,11 @@
     def own(upper_factor):
         return lax.dynamic_slice_in_dim(upper_factor, lax.axis_index("rows") * share_rows, share_rows, 0)
 
-    packed = exchange(matrix, row_signs, all_indices, near, far, room, scale)
+    packed = exchange(matrix, row_signs, samples, near, far, room, scale)
     upper_factor, over = reduce_factor(packed, col_count)
 
     def again():
+        all_indices = lax.all_gather(samples, ("rows", "grp"), axis=0)
         packed = whole_exchange(matrix, row_signs, all_indices, scale)
         return own(reduce_factor(packed, col_count)[0])
 

time: 258 us -> 212 us (0.82)
  blocking collectives: 43.6 us -> 0 us
  other arithmetic: 7.12 us -> 0.7 us
  Pallas kernels: 200 us -> 206 us
    all_gather x1 -> x0, blocking collectives: 43.6 us -> none  [shards(): all_indices = lax.all_gather(samples, ('rows', 'grp'), axis=0)]
    pallas_call x1, Pallas kernels: 108 us -> 117 us  [exchange(): pl.pallas_call(functools.partial(exchange_kernel, (near, far, min(3, step...]
    pallas_call x1, Pallas kernels: 92.1 us -> 89.1 us  [reduce_factor(): call(functools.partial(reduce_factor_kernel, (pair, plane, line)), scratc...]
where the time goes in v3:
time: 212 us
  Pallas kernels  206 us (97%)
  local copies, waits for them, and re-layouts  3.68 us (2%)
    pallas_call x1, Pallas kernels, exchange(): pl.pallas_call(functools.partial(exchange_kernel, (near, far, min(3, step...  117 us
    pallas_call x1, Pallas kernels, reduce_factor(): call(functools.partial(reduce_factor_kernel, (pair, plane, line)), scratc...  89.1 us

profile of v3, /device:TPU:0, one launch (start us, length us, event | category | flops | bytes accessed | tf_op | source)
XLA Modules:
  0.0 211.8 jit_solution(7419089445346137548)
XLA Ops:
  0.0 0.7 convert_element_type.16
  0.7 0.6 reshape.23.s_ref
  1.3 117.3 %shard_map.39.g_ref = f32[5120,128]{1,0:T(8,128)} custom-call(f32[2048,1024]{1,0:T(8,128)} %x_ref.1, f32[8,256]{1,0:T(8,128)} %reshape.23.s_ref, f32[256,256]{1,0:T(8,128)} %constant.110.clone.1.h_ref, s32[2,128]{1,0:T(2,128)} %bitcast.11), custom_call_target="tpu_custom_call" | custom-call | tf_op jit(solution)/shard_map/pallas_call | solution.py:634
  118.6 0.0 copy-start.2
  118.7 0.0 copy-start.3
  118.7 89.1 %shard_map.40 = (f32[1024,1024]{1,0:T(8,128)}, f32[8,128]{1,0:T(8,128)}) custom-call(f32[5120,128]{1,0:T(8,128)} %shard_map.39.g_ref), custom_call_target="tpu_custom_call" | custom-call | tf_op jit(solution)/shard_map/pallas_call | solution.py:380
  207.8 1.2 slice.154
  209.6 0.0 copy-done.2
  209.6 0.0 copy-done.3
  209.6 1.3 conditional.1
  209.7 1.1 constant_dynamic-slice_fusion
  211.0 0.0 copy-start.1
  211.0 0.8 copy-done.1
Async XLA Ops:
  118.6 91.0 %copy-start.2 = (s32[2048]{0:T(1024)S(1)}, s32[2048]{0:T(1024)}, u32[]{:S(2)}) copy-start(s32[2048]{0:T(1024)} %param.6) | copy-start | bytes 24580
  118.7 91.0 %copy-start.3 = (s32[256]{0:T(256)S(1)}, s32[256]{0:T(256)}, u32[]{:S(2)}) copy-start(s32[256]{0:T(256)} %param.7) | copy-start | bytes 3076
  211.0 0.8 copy-start.1

commit v4 on v3

--- a/solution.py
+++ b/solution.py
@@ -10,6 +10,7 @@
 MESH = pl.DeviceIdType.MESH
 VMEM_LIMIT = 60 * 1024 * 1024
 TILE = 128
+AHEAD = 2
 
 
 def sylvester(length):
@@ -121,6 +122,11 @@
 def panel_tiles(panels):
     sizes = [panels - i + (panels - i) % 2 for i in range(panels)]
     return sizes, [sum(sizes[:i]) for i in range(panels)]
+
+
+def column_tiles(panels):
+    sizes = [k + 1 + (k + 1) % 2 for k in range(panels)]
+    return sizes, [sum(sizes[:k]) for k in range(panels)]
 
 
 def segments(panels):
@@ -193,8 +199,8 @@
     return jnp.concatenate(inverse, axis=0)
 
 
-def factor_panels(work, u_ref, lines, high, low):
-    cols = u_ref.shape[0]
+def factor_panels(work, keep, lines, high, low):
+    cols = work.shape[0]
 
     def panel(k, carry):
         base = pl.multiple_of(k * TILE, TILE)
@@ -204,7 +210,7 @@
         wide_lane = lax.broadcasted_iota(jnp.int32, (TILE, cols), 1)
         upper = dot3(lower, split(work[here, :]), ((1,), (0,)))
         upper = jnp.where(wide_lane >= wide_row, upper, 0.0)
-        u_ref[here, :] = upper
+        keep(k, upper)
         high[...], low[...] = split(upper)
 
         def trail(start, i, inner):
@@ -221,6 +227,13 @@
     lax.fori_loop(0, cols // TILE, panel, 0)
 
 
+def keep_all(u_ref):
+    def keep(k, upper):
+        u_ref[pl.ds(pl.multiple_of(k * TILE, TILE), TILE), :] = upper
+
+    return keep
+
+
 def unpack(source, work, panels):
     for i, start in enumerate(panel_tiles(panels)[1]):
         for j in range(i, panels):
@@ -232,7 +245,112 @@
     over_ref[...] = g_ref[g_ref.shape[0] - 8 :, :]
     work[...] = jnp.zeros_like(work)
     unpack(g_ref, work, u_ref.shape[0] // TILE)
-    factor_panels(work, u_ref, lines, high, low)
+    factor_panels(work, keep_all(u_ref), lines, high, low)
+
+
+def reduce_stages(groups, place, runs, g_ref, whole, in1, in2, in3, sum1, sum2, send, arrive):
+    pair, plane, line = groups
+    c, q, b, at = place
+    started = []
+
+    def copy_of(s, stage, t):
+        first, n1, n2, n3 = sizes(s)
+        near1, near2, near3 = first // pair, first // (pair * plane), first // (pair * plane * line)
+        if stage == 0:
+            other = (c + t) % pair
+            source, target, peer = g_ref.at[rows(first + other * n1, n1)], in1.at[t - 1, rows(near1, n1)], at(other, q, b)
+        elif stage == 1:
+            other = (q + t) % plane
+            source, target, peer = sum1.at[rows(near1 + other * n2, n2)], in2.at[t - 1, rows(near2, n2)], at(c, other, b)
+        elif stage == 2:
+            other = (b + t) % line
+            source, target, peer = sum2.at[rows(near2 + other * n3, n3)], in3.at[t - 1, rows(near3, n3)], at(c, q, other)
+        else:
+            if stage == 3:
+                here, peer = rows(first + c * n1 + q * n2 + b * n3, n3), at(c, q, (b + t) % line)
+            elif stage == 4:
+                here, peer = rows(first + c * n1 + q * n2, n2), at(c, (q + t) % plane, b)
+            else:
+                here, peer = rows(first + c * n1, n1), at((c + t) % pair, q, b)
+            source, target = whole.at[here], whole.at[here]
+        slot = stage * 4 + t
+        return pltpu.make_async_remote_copy(
+            src_ref=source,
+            dst_ref=target,
+            send_sem=send.at[s, slot],
+            recv_sem=arrive.at[s, slot],
+            device_id=peer,
+            device_id_type=MESH,
+        )
+
+    counts = [pair, plane, line, line, plane, pair]
+
+    def rows(first, count):
+        return pl.ds(pl.multiple_of(first, 8), count)
+
+    def sizes(s):
+        first, tiles = runs[s]
+        first, n1 = first * TILE, tiles * TILE
+        return first, n1 // pair, n1 // (pair * plane), n1 // (pair * plane * line)
+
+    def start(s, stage):
+        for t in range(1, counts[stage]):
+            copy_of(s, stage, t).start()
+            started.append((s, stage, t))
+
+    def arrived(s, stage):
+        for t in range(1, counts[stage]):
+            copy_of(s, stage, t).wait_recv()
+
+    def scatter1(s):
+        start(s, 0)
+
+    def scatter2(s):
+        first, n1, n2, n3 = sizes(s)
+        mine = rows(first // pair, n1)
+        arrived(s, 0)
+        total = g_ref[rows(first + c * n1, n1), :]
+        for t in range(1, pair):
+            total = total + in1[t - 1, mine, :]
+        sum1[mine, :] = total
+        start(s, 1)
+
+    def scatter3(s):
+        first, n1, n2, n3 = sizes(s)
+        mine = rows(first // (pair * plane), n2)
+        arrived(s, 1)
+        total = sum1[rows(first // pair + q * n2, n2), :]
+        for t in range(1, plane):
+            total = total + in2[t - 1, mine, :]
+        sum2[mine, :] = total
+        start(s, 2)
+
+    def gather3(s):
+        first, n1, n2, n3 = sizes(s)
+        mine = rows(first // (pair * plane * line), n3)
+        arrived(s, 2)
+        total = sum2[rows(first // (pair * plane) + b * n3, n3), :]
+        for t in range(1, line):
+            total = total + in3[t - 1, mine, :]
+        whole[rows(first + c * n1 + q * n2 + b * n3, n3), :] = total
+        start(s, 3)
+
+    def gather2(s):
+        arrived(s, 3)
+        start(s, 4)
+
+    def gather1(s):
+        arrived(s, 4)
+        start(s, 5)
+
+    def finish(s):
+        arrived(s, 5)
+
+    def drain():
+        for item in started:
+            copy_of(*item).wait_send()
+
+    return [scatter1, scatter2, scatter3, gather3, gather2, gather1, finish], drain
 
 
 def reduce_factor_kernel(
@@ -256,101 +374,26 @@
     pl.semaphore_wait(barrier, len(peers))
 
     runs = segments(u_ref.shape[0] // TILE)
-    copies = {}
-
-    def start(s, stage, t, source, target, peer):
-        slot = stage * 4 + t
-        copy = pltpu.make_async_remote_copy(
-            src_ref=source,
-            dst_ref=target,
-            send_sem=send.at[s, slot],
-            recv_sem=arrive.at[s, slot],
-            device_id=peer,
-            device_id_type=MESH,
-        )
-        copy.start()
-        copies[s, stage, t] = copy
-
-    def rows(first, count):
-        return pl.ds(pl.multiple_of(first, 8), count)
-
-    def sizes(s):
-        first, tiles = runs[s]
-        first, n1 = first * TILE, tiles * TILE
-        return first, n1 // pair, n1 // (pair * plane), n1 // (pair * plane * line)
-
-    def scatter1(s):
-        first, n1, n2, n3 = sizes(s)
-        for t in range(1, pair):
-            other = (c + t) % pair
-            start(s, 0, t, g_ref.at[rows(first + other * n1, n1)], in1.at[t - 1, rows(first // pair, n1)], at(other, q, b))
-
-    def scatter2(s):
-        first, n1, n2, n3 = sizes(s)
-        mine = rows(first // pair, n1)
-        total = g_ref[rows(first + c * n1, n1), :]
-        for t in range(1, pair):
-            copies[s, 0, t].wait_recv()
-            total = total + in1[t - 1, mine, :]
-        sum1[mine, :] = total
-        for t in range(1, plane):
-            other = (q + t) % plane
-            start(s, 1, t, sum1.at[rows(first // pair + other * n2, n2)], in2.at[t - 1, rows(first // (pair * plane), n2)], at(c, other, b))
-
-    def scatter3(s):
-        first, n1, n2, n3 = sizes(s)
-        mine = rows(first // (pair * plane), n2)
-        total = sum1[rows(first // pair + q * n2, n2), :]
-        for t in range(1, plane):
-            copies[s, 1, t].wait_recv()
-            total = total + in2[t - 1, mine, :]
-        sum2[mine, :] = total
-        for t in range(1, line):
-            other = (b + t) % line
-            start(s, 2, t, sum2.at[rows(first // (pair * plane) + other * n3, n3)], in3.at[t - 1, rows(first // (pair * plane * line), n3)], at(c, q, other))
-
-    def gather3(s):
-        first, n1, n2, n3 = sizes(s)
-        mine = rows(first // (pair * plane * line), n3)
-        total = sum2[rows(first // (pair * plane) + b * n3, n3), :]
-        for t in range(1, line):
-            copies[s, 2, t].wait_recv()
-            total = total + in3[t - 1, mine, :]
-        here = rows(first + c * n1 + q * n2 + b * n3, n3)
-        whole[here, :] = total
-        for t in range(1, line):
-            start(s, 3, t, whole.at[here], whole.at[here], at(c, q, (b + t) % line))
-
-    def gather2(s):
-        first, n1, n2, n3 = sizes(s)
-        for t in range(1, line):
-            copies[s, 3, t].wait_recv()
-        here = rows(first + c * n1 + q * n2, n2)
-        for t in range(1, plane):
-            start(s, 4, t, whole.at[here], whole.at[here], at(c, (q + t) % plane, b))
-
-    def gather1(s):
-        first, n1, n2, n3 = sizes(s)
-        for t in range(1, plane):
-            copies[s, 4, t].wait_recv()
-        here = rows(first + c * n1, n1)
-        for t in range(1, pair):
-            start(s, 5, t, whole.at[here], whole.at[here], at((c + t) % pair, q, b))
-
-    def finish(s):
-        for t in range(1, pair):
-            copies[s, 5, t].wait_recv()
-
-    stages = [scatter1, scatter2, scatter3, gather3, gather2, gather1, finish]
+    stages, drain = reduce_stages(
+        groups, (c, q, b, at), runs, g_ref, whole, in1, in2, in3, sum1, sum2, send, arrive
+    )
     for step in range(len(runs) + len(stages) - 1):
         for k in reversed(range(len(stages))):
             if 0 <= step - k < len(runs):
                 stages[k](step - k)
-    for copy in copies.values():
-        copy.wait_send()
+    drain()
     over_ref[...] = whole[whole.shape[0] - 8 :, :]
     unpack(whole, work, u_ref.shape[0] // TILE)
-    factor_panels(work, u_ref, lines, high, low)
+    factor_panels(work, keep_all(u_ref), lines, high, low)
+
+
+def reduce_groups(tile_counts):
+    devices = lax.axis_size("rows") * lax.axis_size("grp")
+    pair, plane = 2, 4
+    line = devices // (pair * plane)
+    if devices % (pair * plane) or line != 4 or any(count * TILE % (8 * devices) for count in tile_counts):
+        return None
+    return pair, plane, line
 
 
 def reduce_factor(packed, cols):
@@ -368,17 +411,17 @@
         in_specs=[pl.BlockSpec(memory_space=pltpu.VMEM)],
         out_specs=[pl.BlockSpec(memory_space=pltpu.VMEM)] * 2,
     )
-    pair, plane = 2, 4
-    line = devices // (pair * plane)
-    if devices % (pair * plane) or line > 4 or any(tiles * TILE % (8 * devices) for _, tiles in segments(cols // TILE)):
+    groups = reduce_groups([tiles for _, tiles in segments(cols // TILE)])
+    if not groups:
         return call(
             factor_kernel,
             scratch_shapes=common,
             compiler_params=pltpu.CompilerParams(vmem_limit_bytes=VMEM_LIMIT),
         )(lax.psum(packed, ("rows", "grp")))
+    pair, plane, line = groups
     runs = len(segments(cols // TILE))
     return call(
-        functools.partial(reduce_factor_kernel, (pair, plane, line)),
+        functools.partial(reduce_factor_kernel, groups),
         scratch_shapes=[
             pltpu.VMEM((rows, TILE), jnp.float32),
             pltpu.VMEM((pair - 1, rows // pair, TILE), jnp.float32),
@@ -395,10 +438,15 @@
 
 
 def exchange_kernel(
-    sizes, scale, x_ref, s_ref, h_ref, samples_ref, g_ref,
-    x_in, signed_h, x_out, x_got, mixed, y_out, y_got, high, low, samples, taken, weights, pick_row, pick_ref,
-    load, send_a, got_a, send_b, got_b, send_s, got_s,
+    sizes, scale, groups, x_ref, s_ref, h_ref, samples_ref, *refs
 ):
+    if groups:
+        out_ref, over_ref, g_ref, whole, in1, in2, in3, sum1, sum2, send, arrive, work, spare_lines, row_high, row_low, row_block = refs[:2] + refs[-14:]
+        rest = refs[2:-14]
+    else:
+        g_ref, rest = refs[0], refs[1:]
+    (x_in, signed_h, x_out, x_got, mixed, y_out, y_got, high, low, samples, taken, weights, pick_row, pick_ref,
+    load, send_a, got_a, send_b, got_b, send_s, got_s) = rest
     near, far, ahead = sizes
     steps, rows = x_in.shape[0], x_in.shape[1]
     base, piece, share = h_ref.shape[0], rows // near, weights.shape[0] // far
@@ -462,6 +510,8 @@
             device_id=there,
             device_id_type=MESH,
         )
+
+    flag = TILE if groups else g_ref.shape[0] - 8
 
     def choose():
         lines = samples_ref.shape[0]
@@ -522,7 +572,7 @@
         for kz in range(far):
             here = slice(kz * share, (kz + 1) * share)
             weights[here, :] = weights[here, :] * used
-        g_ref[g_ref.shape[0] - 8 :, :] = jnp.broadcast_to(jnp.where(total > float(room), 1.0, 0.0), (8, TILE))
+        g_ref[flag : flag + 8, :] = jnp.broadcast_to(jnp.where(total > float(room), 1.0, 0.0), (8, TILE))
 
     def transform(c):
         loading(c).wait()
@@ -572,8 +622,12 @@
 
         def gram(i):
             left = pl.ds(pl.multiple_of(i * TILE, TILE), TILE)
-            half = i // 2
-            first = 2 * steps * half - 2 * half * (half - 1) + (i % 2) * (steps - 2 * half)
+            if groups:
+                half = c // 2
+                first = 2 * half * (half + 1) + (c % 2) * (2 * half + 2) + 2 * i - c
+            else:
+                half = i // 2
+                first = 2 * steps * half - 2 * half * (half - 1) + (i % 2) * (steps - 2 * half)
             tile = dot3((high[:, left], low[:, left]), (high[:, lanes], low[:, lanes]), ((0,), (0,)))
             g_ref[span(first + c - i, TILE), :] = tile
 
@@ -589,8 +643,8 @@
     each(1, far, lambda t: greet(at(a, (b + t) % far)))
     for i in range(rows // base):
         signed_h[i] = (h_ref[...] * s_ref[i : i + 1, :]).astype(jnp.bfloat16)
-    sizes_list, starts = panel_tiles(steps)
-    for i in range(1, steps, 2):
+    sizes_list, starts = column_tiles(steps) if groups else panel_tiles(steps)
+    for i in range(0 if groups else 1, steps, 2):
         spare = (starts[i] + sizes_list[i] - 1) * TILE
         g_ref[spare : spare + TILE, :] = jnp.zeros((TILE, TILE), jnp.float32)
     samples[me] = samples_ref[...]
@@ -603,26 +657,72 @@
     each(1, far, lambda t: sample_copy(t, 1).wait_recv())
     choose()
 
+    if groups:
+        pair, plane, line = groups
+
+        def place(cc, qq, bb):
+            return at(qq * pair + cc, bb)
+
+        runs = list(zip(starts, sizes_list))
+        stages, drain = reduce_stages(
+            groups, (a % pair, a // pair, b, place), runs, g_ref, whole, in1, in2, in3, sum1, sum2, send, arrive
+        )
+
+    def stage_at(j, stage, delay):
+        for k in range(steps - delay + 1 if groups else 0):
+            pl.when(j == k + delay)(functools.partial(stages[stage], k))
+
     def step(c):
+        stage_at(c, 1, 2)
+
         @pl.when(c + ahead < steps)
         def _():
             transform(c + ahead)
 
-        middle(c)
+        @pl.when(c < steps)
+        def _():
+            middle(c)
+
+        stage_at(c, 2, 3)
 
         @pl.when(c > 0)
         def _():
             last(c - 1)
 
-    each(0, steps, step)
-    last(steps - 1)
+        stage_at(c, 0, 1)
+        stage_at(c, 3, 4)
+
+    each(0, steps + 1, step)
+    if groups:
+        for wave in range(6):
+            for k in reversed(range(steps)):
+                stage = min(steps - k, 4) + wave
+                if stage < len(stages):
+                    stages[stage](k)
+        over_ref[...] = whole[flag : flag + 8, :]
+        for k, start in enumerate(starts):
+            for i in range(k + 1):
+                tile = (start + i) * TILE
+                work[i * TILE : (i + 1) * TILE, k * TILE : (k + 1) * TILE] = whole[tile : tile + TILE, :]
+        drain()
+        share_rows = out_ref.shape[0]
+        own = lax.axis_index("rows") * share_rows
+
+        def keep_own(k, upper):
+            row_block[...] = upper
+
+            @pl.when(own // TILE == k)
+            def _():
+                out_ref[...] = row_block[pl.ds(pl.multiple_of(own % TILE, 8), share_rows), :]
+
+        factor_panels(work, keep_own, spare_lines, row_high, row_low)
     each(1, near, lambda t: sample_copy(t, 0).wait_send())
     each(1, far, lambda t: sample_copy(t, 1).wait_send())
     each(0, steps, lambda c: each(1, near, lambda t: near_copy(c, t).wait_send()))
     each(0, steps, lambda c: each(1, far, lambda t: far_copy(c, t).wait_send()))
 
 
-def exchange(matrix, row_signs, samples, near, far, room, scale):
+def exchange(matrix, row_signs, samples, near, far, room, scale, groups):
     rows, cols = matrix.shape
     steps = cols // TILE
     base = min(256, rows)
@@ -631,11 +731,34 @@
     tiles = sum(panel_tiles(steps)[0])
     vmem = pl.BlockSpec(memory_space=pltpu.VMEM)
     picks = -(-room // TILE)
+    packed = tiles * TILE
+    gram = jax.ShapeDtypeStruct((packed, TILE), jnp.float32)
+    fused = []
+    if groups:
+        pair, plane, line = groups
+        share_rows = cols // lax.axis_size("rows")
+        outs = [jax.ShapeDtypeStruct((share_rows, cols), jnp.float32), jax.ShapeDtypeStruct((8, TILE), jnp.float32)]
+        fused = [
+            pltpu.VMEM((packed, TILE), jnp.float32),
+            pltpu.VMEM((packed, TILE), jnp.float32),
+            pltpu.VMEM((pair - 1, packed // pair, TILE), jnp.float32),
+            pltpu.VMEM((plane - 1, packed // (pair * plane), TILE), jnp.float32),
+            pltpu.VMEM((max(line - 1, 1), packed // (near * far), TILE), jnp.float32),
+            pltpu.VMEM((packed // pair, TILE), jnp.float32),
+            pltpu.VMEM((packed // (pair * plane), TILE), jnp.float32),
+            pltpu.SemaphoreType.DMA((steps, 24)),
+            pltpu.SemaphoreType.DMA((steps, 24)),
+            pltpu.VMEM((cols, cols), jnp.float32),
+            pltpu.VMEM((2, 10, 8, TILE), jnp.float32),
+            pltpu.VMEM((TILE, cols), jnp.bfloat16),
+            pltpu.VMEM((TILE, cols), jnp.bfloat16),
+            pltpu.VMEM((TILE, cols), jnp.float32),
+        ]
     return pl.pallas_call(
-        functools.partial(exchange_kernel, (near, far, min(3, steps)), scale),
-        out_shape=jax.ShapeDtypeStruct((tiles * TILE, TILE), jnp.float32),
+        functools.partial(exchange_kernel, (near, far, min(AHEAD, steps)), scale, groups),
+        out_shape=outs if groups else gram,
         in_specs=[pl.BlockSpec(memory_space=pl.ANY), vmem, vmem, vmem],
-        out_specs=vmem,
+        out_specs=[vmem, vmem] if groups else vmem,
         scratch_shapes=[
             pltpu.VMEM((steps, rows, TILE), jnp.float32),
             pltpu.VMEM((rows // base, base, base), jnp.bfloat16),
@@ -658,6 +781,7 @@
             pltpu.SemaphoreType.DMA((steps, far)),
             pltpu.SemaphoreType.DMA((near + far,)),
             pltpu.SemaphoreType.DMA((near + far,)),
+            *fused,
         ],
         compiler_params=pltpu.CompilerParams(vmem_limit_bytes=VMEM_LIMIT, collective_id=2, has_side_effects=True),
     )(matrix, row_signs.astype(jnp.float32).reshape(rows // base, base), sylvester(base), padded)
@@ -709,15 +833,20 @@
     def own(upper_factor):
         return lax.dynamic_slice_in_dim(upper_factor, lax.axis_index("rows") * share_rows, share_rows, 0)
 
-    packed = exchange(matrix, row_signs, samples, near, far, room, scale)
-    upper_factor, over = reduce_factor(packed, col_count)
+    groups = reduce_groups([tiles for tiles in column_tiles(col_count // TILE)[0]])
+    if groups:
+        mine, over = exchange(matrix, row_signs, samples, near, far, room, scale, groups)
+    else:
+        packed = exchange(matrix, row_signs, samples, near, far, room, scale, None)
+        upper_factor, over = reduce_factor(packed, col_count)
+        mine = own(upper_factor)
 
     def again():
         all_indices = lax.all_gather(samples, ("rows", "grp"), axis=0)
         packed = whole_exchange(matrix, row_signs, all_indices, scale)
         return own(reduce_factor(packed, col_count)[0])
 
-    return lax.cond(over[0, 0] > 0.0, again, lambda: own(upper_factor))
+    return lax.cond(over[0, 0] > 0.0, again, lambda: mine)
 
 
 def solution(mesh):

time: 212 us -> 195 us (0.920)
  Pallas kernels: 206 us -> 190 us
    pallas_call x2 -> x1, Pallas kernels: 206 us -> 190 us  [exchange(): pl.pallas_call(functools.partial(exchange_kernel, (near, far, min(AHEAD,...]
where the time goes in v4:
time: 195 us
  Pallas kernels  190 us (97%)
  local copies, waits for them, and re-layouts  2.6 us (1%)
    pallas_call x1, Pallas kernels, exchange(): pl.pallas_call(functools.partial(exchange_kernel, (near, far, min(AHEAD,...  190 us

profile of v4, /device:TPU:0, one launch (start us, length us, event | category | flops | bytes accessed | tf_op | source)
XLA Modules:
  0.0 194.5 jit_solution(6545772505596361264)
XLA Ops:
  0.0 0.7 convert_element_type.16
  0.7 0.6 reshape.23.s_ref
  1.3 0.0 copy-start.1
  1.3 0.0 copy-start.2
  1.3 190.3 %shard_map.39 = (f32[128,1024]{1,0:T(8,128)S(1)}, f32[8,128]{1,0:T(8,128)}) custom-call(f32[2048,1024]{1,0:T(8,128)} %x_ref.1, f32[8,256]{1,0:T(8,128)} %reshape.23.s_ref, f32[256,256]{1,0:T(8,128)} %constant.98.clone.1.h_ref, s32[2,128]{1,0:T(2,128)} %bitcast.11), custom_call_target="tpu_custom_call" | custom-call | tf_op jit(solution)/shard_map/pallas_call | solution.py:757
  191.6 1.2 slice.154
  193.5 0.0 copy-done.1
  193.5 0.0 copy-done.2
  193.5 0.2 conditional.1
  193.7 0.8 copy.52
Async XLA Ops:
  1.3 192.2 %copy-start.1 = (s32[2048]{0:T(1024)S(1)}, s32[2048]{0:T(1024)}, u32[]{:S(2)}) copy-start(s32[2048]{0:T(1024)} %param.6) | copy-start | bytes 24580
  1.3 192.2 %copy-start.2 = (s32[256]{0:T(256)S(1)}, s32[256]{0:T(256)}, u32[]{:S(2)}) copy-start(s32[256]{0:T(256)} %param.7) | copy-start | bytes 3076

commit v5 on v4

--- a/solution.py
+++ b/solution.py
@@ -144,7 +144,7 @@
     return jnp.broadcast_to(row, (8, TILE))
 
 def factor_block(block, lines):
-    count, group = TILE // 8, 4
+    count, group = TILE // 8, 8
     sub_id = lax.broadcasted_iota(jnp.int32, (8, TILE), 0)
     lane_id = lax.broadcasted_iota(jnp.int32, (8, TILE), 1)
     strips = [block[8 * i : 8 * i + 8, :] for i in range(count)]
@@ -208,20 +208,24 @@
         lower = split(factor_block(work[here, here], lines))
         wide_row = lax.broadcasted_iota(jnp.int32, (TILE, cols), 0) + base
         wide_lane = lax.broadcasted_iota(jnp.int32, (TILE, cols), 1)
-        upper = dot3(lower, split(work[here, :]), ((1,), (0,)))
+        work_high, work_low = split(work[here, :])
+        left = jnp.concatenate([lower[0], lower[1], lower[0]], axis=1)
+        right = jnp.concatenate([work_high, work_high, work_low], axis=0)
+        upper = jnp.dot(left, right, preferred_element_type=jnp.float32)
         upper = jnp.where(wide_lane >= wide_row, upper, 0.0)
         keep(k, upper)
         high[...], low[...] = split(upper)
 
         def trail(start, i, inner):
             there = pl.ds(pl.multiple_of(i * TILE, TILE), TILE)
-            right = (high[:, start:], low[:, start:])
-            work[there, start:] -= dot3((high[:, there], low[:, there]), right, ((0,), (0,)))
+            left = jnp.concatenate([high[:, there], low[:, there], high[:, there]], axis=0)
+            right = jnp.concatenate([high[:, start:], high[:, start:], low[:, start:]], axis=0)
+            work[there, start:] -= lax.dot_general(left, right, (((0,), (0,)), ((), ())), preferred_element_type=jnp.float32)
             return inner
 
-        half = cols // TILE // 2
-        lax.fori_loop(k + 1, half, functools.partial(trail, 0), 0)
-        lax.fori_loop(jnp.maximum(k + 1, half), cols // TILE, functools.partial(trail, cols // 2), 0)
+        for part in range(4):
+            first, end = part * cols // TILE // 4, (part + 1) * cols // TILE // 4
+            lax.fori_loop(jnp.maximum(k + 1, first), end, functools.partial(trail, first * TILE), 0)
         return carry
 
     lax.fori_loop(0, cols // TILE, panel, 0)

time: 195 us -> 192 us (0.985)
  Pallas kernels: 190 us -> 187 us
    pallas_call x1, Pallas kernels: 190 us -> 187 us  [exchange(): pl.pallas_call(functools.partial(exchange_kernel, (near, far, min(AHEAD,...]
where the time goes in v5:
time: 192 us
  Pallas kernels  187 us (97%)
  local copies, waits for them, and re-layouts  2.6 us (1%)
    pallas_call x1, Pallas kernels, exchange(): pl.pallas_call(functools.partial(exchange_kernel, (near, far, min(AHEAD,...  187 us

profile of v5, /device:TPU:0, one launch (start us, length us, event | category | flops | bytes accessed | tf_op | source)
XLA Modules:
  0.0 191.6 jit_solution(15480420744723612639)
XLA Ops:
  0.0 0.7 convert_element_type.16
  0.7 0.6 reshape.23.s_ref
  1.3 0.0 copy-start.1
  1.3 0.0 copy-start.2
  1.3 187.4 %shard_map.39 = (f32[128,1024]{1,0:T(8,128)S(1)}, f32[8,128]{1,0:T(8,128)}) custom-call(f32[2048,1024]{1,0:T(8,128)} %x_ref.1, f32[8,256]{1,0:T(8,128)} %reshape.23.s_ref, f32[256,256]{1,0:T(8,128)} %constant.98.clone.1.h_ref, s32[2,128]{1,0:T(2,128)} %bitcast.11), custom_call_target="tpu_custom_call" | custom-call | tf_op jit(solution)/shard_map/pallas_call | solution.py:761
  188.7 1.2 slice.154
  190.5 0.0 copy-done.1
  190.6 0.0 copy-done.2
  190.6 0.2 conditional.1
  190.8 0.8 copy.52
Async XLA Ops:
  1.3 189.2 %copy-start.1 = (s32[2048]{0:T(1024)S(1)}, s32[2048]{0:T(1024)}, u32[]{:S(2)}) copy-start(s32[2048]{0:T(1024)} %param.6) | copy-start | bytes 24580
  1.3 189.3 %copy-start.2 = (s32[256]{0:T(256)S(1)}, s32[256]{0:T(256)}, u32[]{:S(2)}) copy-start(s32[256]{0:T(256)} %param.7) | copy-start | bytes 3076
